TPU v7x, 32 devices: a whole 2x2x4 slice. The times are simulated.
32 devices in a mesh: dp: 8 (over y, x, core), mp: 4 (over z).
Axes of the slice: x: 2, y: 2, z: 4, core: 2. Of those that a mesh axis runs over, the one named last changes fastest.
Arguments:
- inputs: bfloat16 [1024, 6144], P('dp'), may hold values from -6 to 6
- pre_act: bfloat16 [1024, 12288], P('dp', 'mp'), may hold values from -6 to 6
- out_grad: bfloat16 [1024, 6144], P('dp'), may hold values from -6 to 6
- w_in: bfloat16 [6144, 12288], P(None, 'mp'), may hold values from -0.109375 to 0.109375
- w_out: bfloat16 [12288, 6144], P('mp'), may hold values from -0.0546875 to 0.0546875
- master_in: float32 [6144, 12288], P('dp', 'mp'), may hold values from -0.3 to 0.3
- master_out: float32 [12288, 6144], P('mp', 'dp'), may hold values from -0.3 to 0.3
- row_in: float32 [6144], P('dp'), may hold values from 12.8 to 686.08
- col_in: float32 [12288], P('mp'), may hold values from 25 to 128
- row_out: float32 [12288], P('mp'), may hold values from 25.6 to 1372.16
- col_out: float32 [6144], P('dp'), may hold values from 51 to 256
Outputs:
- input_grad: bfloat16 [1024, 6144], P('dp', 'mp')
- new_master_in: float32 [6144, 12288], P('dp', 'mp')
- new_master_out: float32 [12288, 6144], P('mp', 'dp')
All inputs are finite; a program needn't handle non-finite values.
Results may differ from a plain program's by a relative error of at most 0.012.
Values may be sent and summed in bfloat16 or wider, within the bound.
A program may use at most 256 MiB of HBM per device.

v0:
```python
import math

import jax
import jax.numpy as jnp
from jax import lax
from jax.experimental.layout import Layout, with_layout_constraint
from jax.sharding import PartitionSpec as P

D = 6144
FF = 12288


decay_rate = 0.8
step_size = 0.05
tiny_square = 1e-30


def gelu_parts(pre):
    cumulative = 0.5 * (1.0 + jax.scipy.special.erf(pre * (1.0 / math.sqrt(2.0))))
    density = jnp.exp(-0.5 * pre * pre) * (1.0 / math.sqrt(2.0 * math.pi))
    return (pre * cumulative, cumulative + pre * density)


def contract_rows(left, right):
    return lax.dot_general(
        left, right, (((0,), (0,)), ((), ())), preferred_element_type=jnp.float32
    )


def scatter_pieces(partial, axis):
    size = lax.axis_size(axis)
    me = lax.axis_index(axis)
    width = partial.shape[1] // size
    piece = lambda k: lax.dynamic_slice_in_dim(partial, k * width, width, 1)
    pieces = [piece(me)]
    for shift in range(1, size):
        moved = piece(lax.rem(me + shift, size)).astype(jnp.bfloat16)
        pieces.append(lax.ppermute(moved, axis, [(i, (i + shift) % size) for i in range(size)]))
    return pieces


def body(
    inputs, pre_act, out_grad, w_in, w_out, master_in, master_out, row_in, col_in, row_out, col_out
):
    active, slope = gelu_parts(pre_act.astype(jnp.float32))
    hidden = active.astype(jnp.bfloat16)
    hidden_all = lax.all_gather(hidden, "dp", axis=0, tiled=True)
    out_grad, _ = lax.optimization_barrier((out_grad, hidden))
    out_cols = lax.all_to_all(out_grad, "dp", 1, 0, tiled=True)
    hid_grad = lax.dot_general(
        out_grad, w_out, (((1,), (1,)), ((), ())), preferred_element_type=jnp.float32
    )
    pre_grad = (hid_grad * slope).astype(jnp.bfloat16)
    pre_grad_all = lax.all_gather(pre_grad, "dp", axis=0, tiled=True)
    input_part = lax.dot_general(
        pre_grad, w_in, (((1,), (1,)), ((), ())), preferred_element_type=jnp.float32
    )
    inputs, input_part = lax.optimization_barrier((inputs, input_part))
    in_cols = lax.all_to_all(inputs, "dp", 1, 0, tiled=True)
    pieces = scatter_pieces(input_part, "mp")

    grad_out = contract_rows(hidden_all, out_cols)
    square_out = grad_out * grad_out + tiny_square
    width_out, row_out_sum = lax.psum((jnp.sum(square_out, axis=0), jnp.sum(row_out)), "mp")
    cols_out = decay_rate * col_out + (1.0 - decay_rate) * width_out / FF
    hidden_out, sum_out = lax.psum((jnp.sum(square_out, axis=1), jnp.sum(width_out)), "dp")
    rows_out = decay_rate * row_out + (1.0 - decay_rate) * hidden_out / D
    mean_out = (decay_rate * row_out_sum + (1.0 - decay_rate) * sum_out / D) / FF
    update_out = grad_out / jnp.sqrt(rows_out[:, None] * cols_out[None, :] / mean_out)
    new_master_out = master_out - step_size * update_out

    pre_grad_all, new_master_out, pieces = lax.optimization_barrier(
        (pre_grad_all, new_master_out, pieces)
    )
    input_grad = sum(piece.astype(jnp.float32) for piece in pieces).astype(jnp.bfloat16)
    grad_in = with_layout_constraint(contract_rows(in_cols, pre_grad_all), Layout((0, 1)))
    square_in = grad_in * grad_in + tiny_square
    width_in = lax.psum(jnp.sum(square_in, axis=1), "mp")
    rows_in = decay_rate * row_in + (1.0 - decay_rate) * width_in / FF
    hidden_in, sum_in = lax.psum((jnp.sum(square_in, axis=0), jnp.sum(rows_in)), "dp")
    cols_in = decay_rate * col_in + (1.0 - decay_rate) * hidden_in / D
    mean_in = sum_in / D
    update_in = grad_in / jnp.sqrt(rows_in[:, None] * cols_in[None, :] / mean_in)
    new_master_in = master_in - step_size * update_in
    return (input_grad, new_master_in, new_master_out)


def solution(mesh):
    in_specs = (
        P("dp", None),
        P("dp", "mp"),
        P("dp", None),
        P(None, "mp"),
        P("mp", None),
        P("dp", "mp"),
        P("mp", "dp"),
        P("dp"),
        P("mp"),
        P("mp"),
        P("dp"),
    )
    out_specs = (P("dp", "mp"), P("dp", "mp"), P("mp", "dp"))
    return jax.shard_map(body, mesh=mesh, in_specs=in_specs, out_specs=out_specs, check_vma=False)
```

profile of v0, /device:TPU:0, one launch (start us, length us, event | category | flops | bytes accessed | tf_op | source)
XLA Modules:
  0.0 233.9 jit_solution(13261236055143968567)
XLA Ops:
  7.2 0.0 all-gather.5.cloned.1.call-start
  7.2 2.4 %fusion.8 = bf16[128,3072]{1,0:T(8,128)(2,1)} fusion(bf16[128,3072]{1,0:T(8,128)(2,1)} %param.12), kind=kLoop, calls=%fused_computation.18 | loop fusion | flops 2359296 | bytes 1572864 | tf_op jit(solution)/shard_map/convert_element_type | solution.py:46
  9.6 0.0 all-gather.5.cloned.1.call-update
  9.6 0.0 all-gather.3.cloned.1.call-start
  9.7 22.5 %fusion.4 = bf16[128,3072]{1,0:T(8,128)(2,1)} fusion(bf16[128,6144]{1,0:T(8,128)(2,1)} %param.13, bf16[3072,6144]{1,0:T(8,128)(2,1)} %param.15, bf16[128,3072]{1,0:T(8,128)(2,1)} %param.12), kind=kOutput, calls=%fused_computation.9 | convolution fusion | flops 4836163584 | bytes 40894464 | tf_op jit(solution)/shard_map/dot_general | solution.py:50
  32.2 1.6 copy.14
  33.8 5.2 %all-to-all-start = ((bf16[128,8,768]{0,2,1:T(8,128)(2,1)}), bf16[128,8,768]{0,2,1:T(8,128)(2,1)}, u32[]{:S(2)}, u32[]{:S(2)}) async-start(bf16[128,8,768]{0,2,1:T(8,128)(2,1)} %bitcast), calls=%async_computation | async-start | bytes 3145728 | tf_op jit(solution)/shard_map/all_to_all | solution.py:49
  39.0 17.9 %fusion.13 = f32[128,6144]{1,0:T(8,128)S(1)} fusion(bf16[128,3072]{1,0:T(8,128)(2,1)} %fusion.4, bf16[6144,3072]{1,0:T(8,128)(2,1)} %param.14), kind=kOutput, calls=%fused_computation.32 | convolution fusion | flops 4831838208 | bytes 41680896 | tf_op jit(solution)/shard_map/dot_general | solution.py:55
  57.0 2.6 %copy.16 = bf16[128,6144]{0,1:T(8,128)(2,1)} copy(bf16[128,6144]{1,0:T(8,128)(2,1)} %param.11) | data formatting | bytes 3145728 | tf_op jit(solution)/shard_map/optimization_barrier | solution.py:58
  59.5 14.5 %all-to-all-done = bf16[128,8,768]{0,2,1:T(8,128)(2,1)} async-done(((bf16[128,8,768]{0,2,1:T(8,128)(2,1)}), bf16[128,8,768]{0,2,1:T(8,128)(2,1)}, u32[]{:S(2)}, u32[]{:S(2)}) %all-to-all-start) | async-done | bytes 1572896 | tf_op jit(solution)/shard_map/all_to_all | solution.py:49
  74.1 4.3 %all-to-all-start.1 = ((bf16[128,8,768]{0,2,1:T(8,128)(2,1)}), bf16[128,8,768]{0,2,1:T(8,128)(2,1)}, u32[]{:S(2)}, u32[]{:S(2)}) async-start(bf16[128,8,768]{0,2,1:T(8,128)(2,1)} %bitcast.14), calls=%async_computation.1 | async-start | bytes 3145728 | tf_op jit(solution)/shard_map/all_to_all | solution.py:59
  78.4 1.1 dynamic-slice_convert_fusion
  79.4 3.3 %collective-permute-start.2 = (bf16[128,1536]{1,0:T(8,128)(2,1)}, bf16[128,1536]{1,0:T(8,128)(2,1)S(1)}, u32[]{:S(2)}, u32[]{:S(2)}) collective-permute-start(bf16[128,1536]{1,0:T(8,128)(2,1)} %get-tuple-element.33), channel_id=1, source_target_pairs={{0,3},{1,0},{2,1},{3,2},{4,7},{5,4},{6,5},{7,6},{8,11},{9,8},{10,9... | collective-permute-start | bytes 1179656 | tf_op jit(solution)/shard_map/ppermute | solution.py:38
  82.8 1.1 collective-permute-start
  83.9 0.6 reduce_sum.65
  84.5 1.0 constant_dynamic-slice_fusion
  85.4 2.6 %copy.15 = bf16[8,128,768]{2,1,0:T(8,128)(2,1)} copy(bf16[8,128,768]{1,2,0:T(8,128)(2,1)} %bitcast.1) | data formatting | bytes 3145728 | tf_op jit(solution)/shard_map/all_to_all | solution.py:49
  88.0 19.7 %all-to-all-done.1 = bf16[128,8,768]{0,2,1:T(8,128)(2,1)} async-done(((bf16[128,8,768]{0,2,1:T(8,128)(2,1)}), bf16[128,8,768]{0,2,1:T(8,128)(2,1)}, u32[]{:S(2)}, u32[]{:S(2)}) %all-to-all-start.1) | async-done | bytes 1572896 | tf_op jit(solution)/shard_map/all_to_all | solution.py:59
  107.7 1.7 copy.17
  109.5 0.0 all-gather.5.cloned.1.call-done
  109.5 10.4 %fusion.1 = (f32[3072]{0:T(1024)S(1)}, f32[768]{0:T(1024)S(1)}, f32[3072,768]{1,0:T(8,128)}) fusion(bf16[1024,3072]{1,0:T(8,128)(2,1)} %all-gather.5.cloned.1.call-done, bf16[1024,768]{1,0:T(8,128)(2,1)} %bitcast.16), kind=kOutput, calls=%fused_computation.5 | convolution fusion | flops 4841271296 | bytes 17316864 | tf_op jit(solution)/shard_map/dot_general | solution.py:25
  119.9 12.4 %all-reduce.2 = (f32[]{:T(128)}, f32[768]{0:T(1024)S(1)}) all-reduce(f32[]{:T(128)} %reduce_sum.65, f32[768]{0:T(1024)S(1)} %get-tuple-element.24), channel_id=1, replica_groups=mesh['dp'=8,'mp'=4] {'mp'}, use_global_device_ids=true, to_apply=%region_5.0 | all-reduce | flops 769 | bytes 6152 | tf_op jit(solution)/shard_map/psum | solution.py:64
  132.4 0.6 multiply_add_fusion.5
  133.0 23.4 %all-reduce.1 = (f32[]{:T(128)}, f32[3072]{0:T(1024)S(1)}) all-reduce(f32[]{:T(128)} %get-tuple-element.37, f32[3072]{0:T(1024)S(1)} %get-tuple-element.23), channel_id=1, replica_groups=mesh['dp'=8,'mp'=4] {'dp'}, use_global_device_ids=true, to_apply=%region_7.0 | all-reduce | flops 3073 | bytes 24584 | tf_op jit(solution)/shard_map/psum | solution.py:66
  157.7 11.2 %multiply_subtract_fusion.1 = f32[3072,768]{1,0:T(8,128)} fusion(f32[3072,768]{1,0:T(8,128)} %param.17, f32[3072,768]{1,0:T(8,128)} %get-tuple-element.38, f32[]{:T(128)S(6)} %div.48, f32[768]{0:T(1024)S(1)} %get-tuple-element.36, f32[3072]{0:T(1024)S(1)} %multiply_add_fusion.3), kind=kLoop, calls=%fused_computation.2 | loop fusion | flops 11796480 | bytes 28326916 | tf_op jit(solution)/shard_map/sub | solution.py:70
  169.0 0.0 all-gather.3.cloned.1.call-done
  169.0 11.3 %fusion.2 = (f32[3072]{0:T(1024)S(1)}, f32[768]{0:T(1024)S(1)}, f32[768,3072]{1,0:T(8,128)}) fusion(bf16[1024,768]{1,0:T(8,128)(2,1)S(1)} %bitcast.15, bf16[1024,3072]{1,0:T(8,128)(2,1)} %all-gather.3.cloned.1.call-done), kind=kOutput, calls=%fused_computation.6 | convolution fusion | flops 4841271296 | bytes 17316864 | tf_op jit(solution)/shard_map/dot_general | solution.py:25
  180.3 8.3 %psum.53 = f32[768]{0:T(1024)S(1)} all-reduce(f32[768]{0:T(1024)S(1)} %get-tuple-element.22), channel_id=1, replica_groups=mesh['dp'=8,'mp'=4] {'mp'}, use_global_device_ids=true, to_apply=%region_9.0 | all-reduce | flops 768 | bytes 6144 | tf_op jit(solution)/shard_map/psum | solution.py:78
  188.6 0.6 fusion.12
  189.2 23.4 %all-reduce = (f32[]{:T(128)}, f32[3072]{0:T(1024)S(1)}) all-reduce(f32[]{:T(128)} %get-tuple-element.31, f32[3072]{0:T(1024)S(1)} %get-tuple-element.21), channel_id=1, replica_groups=mesh['dp'=8,'mp'=4] {'dp'}, use_global_device_ids=true, to_apply=%region_13.0 | all-reduce | flops 3073 | bytes 24584 | tf_op jit(solution)/shard_map/psum | solution.py:80
  213.3 2.0 add_convert_fusion
  215.3 11.7 %multiply_subtract_fusion = f32[768,3072]{1,0:T(8,128)} fusion(f32[768,3072]{1,0:T(8,128)} %param.16, f32[768,3072]{1,0:T(8,128)} %get-tuple-element.39, f32[]{:T(128)S(6)} %div.54, f32[3072]{0:T(1024)S(1)} %multiply_add_fusion.2, f32[768]{0:T(1024)S(1)} %get-tuple-element.32), kind=kLoop, calls=%fused_computation | loop fusion | flops 11796480 | bytes 28326916 | tf_op jit(solution)/shard_map/sub | solution.py:84
  (19 shorter events, 0.1 us)
Async XLA Ops:
  7.2 102.3 %all-gather.5.cloned.1.call-start = ((), (), s32[]{:S(2)}) async-start(), calls=%async_computation.3 | async-start | bytes 7077888 | tf_op jit(solution)/shard_map/all_gather | solution.py:47
  9.6 22.6 %copy-start.1 = (bf16[128,6144]{1,0:T(8,128)(2,1)S(1)}, bf16[128,6144]{1,0:T(8,128)(2,1)}, u32[]{:S(2)}) copy-start(bf16[128,6144]{1,0:T(8,128)(2,1)} %param.13) | copy-start | bytes 4718596
  9.6 159.4 %all-gather.3.cloned.1.call-start = ((), (), s32[]{:S(2)}) async-start(), calls=%async_computation.2 | async-start | bytes 7077888 | tf_op jit(solution)/shard_map/all_gather | solution.py:54
  33.8 40.2 %all-to-all-start = ((bf16[128,8,768]{0,2,1:T(8,128)(2,1)}), bf16[128,8,768]{0,2,1:T(8,128)(2,1)}, u32[]{:S(2)}, u32[]{:S(2)}) async-start(bf16[128,8,768]{0,2,1:T(8,128)(2,1)} %bitcast), calls=%async_computation | async-start | bytes 3145728 | tf_op jit(solution)/shard_map/all_to_all | solution.py:49
  56.9 26.9 %copy-start.2 = (f32[3072]{0:T(1024)S(1)}, f32[3072]{0:T(1024)}, u32[]{:S(2)}) copy-start(f32[3072]{0:T(1024)} %param.20) | copy-start | bytes 36868
  74.1 33.7 %all-to-all-start.1 = ((bf16[128,8,768]{0,2,1:T(8,128)(2,1)}), bf16[128,8,768]{0,2,1:T(8,128)(2,1)}, u32[]{:S(2)}, u32[]{:S(2)}) async-start(bf16[128,8,768]{0,2,1:T(8,128)(2,1)} %bitcast.14), calls=%async_computation.1 | async-start | bytes 3145728 | tf_op jit(solution)/shard_map/all_to_all | solution.py:59
  79.4 89.5 %collective-permute-start.2 = (bf16[128,1536]{1,0:T(8,128)(2,1)}, bf16[128,1536]{1,0:T(8,128)(2,1)S(1)}, u32[]{:S(2)}, u32[]{:S(2)}) collective-permute-start(bf16[128,1536]{1,0:T(8,128)(2,1)} %get-tuple-element.33), channel_id=1, source_target_pairs={{0,3},{1,0},{2,1},{3,2},{4,7},{5,4},{6,5},{7,6},{8,11},{9,8},{10,9... | collective-permute-start | bytes 1179656 | tf_op jit(solution)/shard_map/ppermute | solution.py:38
  82.8 86.2 %collective-permute-start.1 = (bf16[128,1536]{1,0:T(8,128)(2,1)}, bf16[128,1536]{1,0:T(8,128)(2,1)}, u32[]{:S(2)}, u32[]{:S(2)}) collective-permute-start(bf16[128,1536]{1,0:T(8,128)(2,1)} %get-tuple-element.34), channel_id=1, source_target_pairs={{0,2},{1,3},{2,0},{3,1},{4,6},{5,7},{6,4},{7,5},{8,10},{9,11},{10,... | collective-permute-start | bytes 1179656 | tf_op jit(solution)/shard_map/ppermute | solution.py:38
  82.8 86.2 %collective-permute-start = (bf16[128,1536]{1,0:T(8,128)(2,1)}, bf16[128,1536]{1,0:T(8,128)(2,1)}, u32[]{:S(2)}, u32[]{:S(2)}) collective-permute-start(bf16[128,1536]{1,0:T(8,128)(2,1)} %get-tuple-element.35), channel_id=1, source_target_pairs={{0,1},{1,2},{2,3},{3,0},{4,5},{5,6},{6,7},{7,4},{8,9},{9,10},{10,1... | collective-permute-start | bytes 1179656 | tf_op jit(solution)/shard_map/ppermute | solution.py:38
  109.5 22.9 %copy-start.4 = (f32[768]{0:T(1024)S(1)}, f32[768]{0:T(1024)}, u32[]{:S(2)}) copy-start(f32[768]{0:T(1024)} %param.21) | copy-start | bytes 9220
  169.0 19.6 %copy-start.5 = (f32[768]{0:T(1024)S(1)}, f32[768]{0:T(1024)}, u32[]{:S(2)}) copy-start(f32[768]{0:T(1024)} %param.18) | copy-start | bytes 9220
  169.0 44.2 %copy-start.3 = (f32[3072]{0:T(1024)S(1)}, f32[3072]{0:T(1024)}, u32[]{:S(2)}) copy-start(f32[3072]{0:T(1024)} %param.19) | copy-start | bytes 36868
  169.0 44.2 %copy-start = (f32[128,1536]{1,0:T(8,128)S(1)}, f32[128,1536]{1,0:T(8,128)}, u32[]{:S(2)}) copy-start(f32[128,1536]{1,0:T(8,128)} %constant_dynamic-slice_fusion) | copy-start | bytes 2359300
Sparse Core Ops, SparseCore 0:
  9.9 61.8 all-gather.4
  73.7 59.2 all-gather.2
where the time goes:
time: 234 us
  blocking collectives  67.5 us (29%)
  matrix products  62.1 us (27%)
  waiting for transfers between devices  34.3 us (15%)
  other arithmetic  29.2 us (12%)
  between operations  16.2 us (7%)
  starting transfers between devices  14 us (6%)
  local copies, waits for them, and re-layouts  10.5 us (4%)
    psum x1, blocking collectives, body(): lax.psum((jnp.sum(square_out, axis=1), jnp.sum(width_out)), 'dp')  23.4 us
    psum x1, blocking collectives, body(): lax.psum((jnp.sum(square_in, axis=0), jnp.sum(rows_in)), 'dp')  23.4 us
    dot_general x1, matrix products, body(): lax.dot_general(out_grad, w_out, (((1,), (1,)), ((), ())), preferred_elem...  22.5 us
    dot_general x2, matrix products, contract_rows(): lax.dot_general(left, right, (((0,), (0,)), ((), ())), preferred_element_...  21.7 us
    all_to_all x1, waiting for transfers between devices, body(): in_cols = lax.all_to_all(inputs, 'dp', 1, 0, tiled=True)  19.7 us
    dot_general x1, matrix products, body(): lax.dot_general(pre_grad, w_in, (((1,), (1,)), ((), ())), preferred_eleme...  17.9 us
    all_to_all x1, waiting for transfers between devices, body(): out_cols = lax.all_to_all(out_grad, 'dp', 1, 0, tiled=True)  14.5 us
    psum x1, blocking collectives, body(): lax.psum((jnp.sum(square_out, axis=0), jnp.sum(row_out)), 'mp')  12.4 us
  transfers between devices with their start and end apart: 7, of which 2 were waited for; matrix products, arithmetic and copies ran while one was open for 32% of the time, Pallas kernels for 0%

commit v1 on v0

--- a/solution.py
+++ b/solution.py
@@ -1,8 +1,11 @@
+import functools
 import math
 
 import jax
 import jax.numpy as jnp
 from jax import lax
+from jax.experimental import pallas as pl
+from jax.experimental.pallas import tpu as pltpu
 from jax.experimental.layout import Layout, with_layout_constraint
 from jax.sharding import PartitionSpec as P
 
@@ -83,6 +86,456 @@
     update_in = grad_in / jnp.sqrt(rows_in[:, None] * cols_in[None, :] / mean_in)
     new_master_in = master_in - step_size * update_in
     return (input_grad, new_master_in, new_master_out)
+
+
+MESH = pl.DeviceIdType.MESH
+NT = (((1,), (1,)), ((), ()))
+NN = (((1,), (0,)), ((), ()))
+LANES = 128
+
+
+def dot(left, right, dims):
+    return lax.dot_general(left, right, dims, preferred_element_type=jnp.float32)
+
+
+class Copies:
+    def __init__(self, sems):
+        self.sems = sems
+        self.count = 0
+        self.sent = []
+
+    def take(self, number=1):
+        first = self.count
+        self.count += number
+        return first
+
+    def local(self, src, dst):
+        copy = pltpu.make_async_copy(src, dst, self.sems.at[self.take()])
+        copy.start()
+        return copy
+
+    def remote(self, src, dst, recv, **device):
+        copy = pltpu.make_async_remote_copy(
+            src_ref=src,
+            dst_ref=dst,
+            send_sem=self.sems.at[self.take()],
+            recv_sem=self.sems.at[recv],
+            device_id=device,
+            device_id_type=MESH,
+        )
+        copy.start()
+        self.sent.append(copy)
+
+    def arrived(self, dst, recv, **device):
+        pltpu.make_async_remote_copy(
+            src_ref=dst,
+            dst_ref=dst,
+            send_sem=self.sems.at[recv],
+            recv_sem=self.sems.at[recv],
+            device_id=device,
+            device_id_type=MESH,
+        ).wait_recv()
+
+    def drain(self):
+        for copy in self.sent:
+            copy.wait_send()
+
+
+def step_kernel(
+    plan,
+    og_hbm, pa_hbm, in_hbm, wo_hbm, wi_hbm, row_out, col_out, row_in, col_in,
+    ig_ref, go_hbm, gi_hbm, fro_ref, fco_ref, fri_ref, fci_ref,
+    og2, pa2, hid, pre, oc, ic, ict, wob, wib, ipb, rpb, go, gi, racc,
+    vec_d, vec_m, sems, local_sems,
+):
+    n_dp, n_mp, tok, width, ff, cols, parts = plan
+    half, depth = ff // 2, width // 2
+    piece = width // n_mp
+    chunk = half // parts
+    d, z = lax.axis_index("dp"), lax.axis_index("mp")
+    core, chip = lax.rem(d, 2), d // 2
+    base = pl.multiple_of(chip * 2 * tok, 2 * tok)
+    flip = lambda index: d + sum(
+        bit * (1 - 2 * lax.rem(d // bit, 2)) for bit in (1, 2, 4) if index & bit
+    )
+    turn = lambda index: z + sum(
+        bit * (1 - 2 * lax.rem(z // bit, 2)) for bit in (1, 2) if index & bit
+    )
+    dp_of = {index: flip(index) for index in range(1, n_dp)}
+    mp_of = {index: turn(index) for index in range(1, n_mp)}
+    on = lambda index: dict(dp=dp_of[index], mp=z)
+
+    barrier = pltpu.get_barrier_semaphore()
+    for index in range(1, n_dp):
+        pl.semaphore_signal(barrier, inc=1, device_id=on(index), device_id_type=MESH)
+    for index in range(1, n_mp):
+        for peer in (d, dp_of[1]):
+            device = dict(dp=peer, mp=mp_of[index])
+            pl.semaphore_signal(barrier, inc=1, device_id=device, device_id_type=MESH)
+
+    c = Copies(sems)
+    rows_of = lambda who: pl.ds(pl.multiple_of(who * tok, tok), tok)
+    mine = pl.ds(pl.multiple_of(core * tok, tok), tok)
+    other = pl.ds(pl.multiple_of((1 - core) * tok, tok), tok)
+    half_cols = lambda which: pl.ds(pl.multiple_of(which * half, half), half)
+    start = [
+        c.local(pa_hbm.at[:, half_cols(core)], pa2.at[mine]),
+        c.local(og_hbm, og2.at[mine]),
+    ]
+    own_cols = pl.ds(pl.multiple_of(d * cols, cols), cols)
+    own_oc = c.local(og_hbm.at[:, own_cols], oc.at[rows_of(d)])
+    own_ic = c.local(in_hbm.at[:, own_cols], ic.at[rows_of(d)])
+
+    n_out = half // chunk
+    slots = wob.shape[0]
+    wo_copy = lambda k: pltpu.make_async_copy(
+        wo_hbm.at[pl.ds(pl.multiple_of(core * half + k * chunk, chunk), chunk)],
+        wob.at[k % slots],
+        local_sems.at[k % slots],
+    )
+    in_rows = wib.shape[1]
+    n_in = depth // in_rows
+    wi_copy = lambda k: pltpu.make_async_copy(
+        wi_hbm.at[pl.ds(pl.multiple_of(core * depth + k * in_rows, in_rows), in_rows)],
+        wib.at[k % slots],
+        local_sems.at[slots + k % slots],
+    )
+    for k in range(slots):
+        wo_copy(k).start()
+
+    pl.semaphore_wait(barrier, n_dp - 1 + 2 * (n_mp - 1))
+
+    r_pa, r_og = c.take(), c.take()
+    c.remote(pa_hbm.at[:, half_cols(1 - core)], pa2.at[mine], r_pa, **on(1))
+    c.remote(og_hbm, og2.at[mine], r_og, **on(1))
+
+    r_oc, r_ic = c.take(n_dp), c.take(n_dp)
+
+    def spread(src, dst, recv):
+        for index in (2, 4, 6, 3, 5, 7, 1):
+            who = dp_of[index]
+            their = pl.ds(pl.multiple_of(who * cols, cols), cols)
+            c.remote(src.at[:, their], dst.at[rows_of(d)], recv + index, **on(index))
+
+    def gathered(dst, recv):
+        for index in range(1, n_dp):
+            c.arrived(dst.at[rows_of(dp_of[index])], recv + index, **on(index))
+
+    spread(og_hbm, oc, r_oc)
+
+    def block(dst, index, which, k):
+        tokens = pl.ds(pl.multiple_of((dp_of[index] if index else d) // 2 * 2 * tok, 2 * tok), 2 * tok)
+        units = pl.ds(pl.multiple_of(which * half + k * chunk, chunk), chunk)
+        return dst.at[units, tokens] if dst is hid else dst.at[tokens, units]
+
+    r_h, r_p = {}, {}
+    for table in (r_h, r_p):
+        for index in (0, 2, 4, 6):
+            table[index] = c.take(parts), c.take(parts)
+
+    def send_own(dst, table, k):
+        src = block(dst, 0, core, k)
+        c.remote(src, src, table[2][0] + k, **on(2))
+        c.remote(src, src, table[4][0] + k, **on(4))
+        c.remote(src, src, table[0][1] + k, **on(1))
+
+    def pass_on(dst, table, index, k):
+        src = block(dst, index, core, k)
+        c.arrived(src, table[index][0] + k, **on(index))
+        if index == 2 and k < parts // 2:
+            c.remote(src, src, table[6][0] + k, **on(4))
+        if index == 4 and k >= parts // 2:
+            c.remote(src, src, table[6][0] + k, **on(2))
+        c.remote(src, src, table[index][1] + k, **on(1))
+
+    def from_partner(dst, table, index, k):
+        c.arrived(block(dst, index, 1 - core, k), table[index][1] + k, **on(1))
+
+    for copy in start:
+        copy.wait()
+    c.arrived(pa2.at[other], r_pa, **on(1))
+
+    for k in range(parts):
+        units = slice(k * chunk, (k + 1) * chunk)
+        active, _ = gelu_parts(pa2[:, units].astype(jnp.float32))
+        target = pl.ds(pl.multiple_of(core * half + k * chunk, chunk), chunk)
+        hid[target, pl.ds(base, 2 * tok)] = active.T.astype(jnp.bfloat16)
+        if k:
+            send_own(hid, r_h, k - 1)
+    c.arrived(og2.at[other], r_og, **on(1))
+    for k in range(n_in if n_in < slots else slots):
+        wi_copy(k).start()
+    for k in range(parts):
+        wo_copy(k).wait()
+        hid_grad = dot(og2[...], wob[k % slots], NT)
+        _, slope = gelu_parts(pa2[:, k * chunk : (k + 1) * chunk].astype(jnp.float32))
+        target = pl.ds(pl.multiple_of(core * half + k * chunk, chunk), chunk)
+        pre[pl.ds(base, 2 * tok), target] = (hid_grad * slope).astype(jnp.bfloat16)
+        if k + slots < n_out:
+            wo_copy(k + slots).start()
+        if k:
+            send_own(pre, r_p, k - 1)
+        else:
+            send_own(hid, r_h, parts - 1)
+            spread(in_hbm, ic, r_ic)
+    for k in range(parts - 1):
+        from_partner(pre, r_p, 0, k)
+    send_own(pre, r_p, parts - 1)
+    from_partner(pre, r_p, 0, parts - 1)
+
+    r_rp = c.take(n_mp)
+    owned = n_mp // 2
+    s_rp = c.take(owned * 2)
+
+    def piece_copy(which, t):
+        to = core * owned + which
+        return pltpu.make_async_remote_copy(
+            src_ref=ipb.at[which, pl.ds(t * tok, tok)],
+            dst_ref=rpb.at[z],
+            send_sem=sems.at[s_rp + which * 2 + t],
+            recv_sem=sems.at[r_rp + z],
+            device_id=dict(dp=chip * 2 + t, mp=to),
+            device_id_type=MESH,
+        ), jnp.logical_or(to != z, core != t)
+
+    def send_pieces(which):
+        for t in range(2):
+            copy, away = piece_copy(which, t)
+
+            @pl.when(away)
+            def _():
+                copy.start()
+
+    per = n_in // owned
+    for k in range(n_in):
+        wi_copy(k).wait()
+        part = dot(pre[pl.ds(base, 2 * tok), :], wib[k % slots], NT)
+        ipb[k // per, :, k % per * in_rows : (k % per + 1) * in_rows] = part.astype(jnp.bfloat16)
+        if k + slots < n_in:
+            wi_copy(k + slots).start()
+        if k and k % per == 0:
+            send_pieces(k // per - 1)
+
+    own_ic.wait()
+    own_oc.wait()
+    gathered(oc, r_oc)
+    send_pieces(owned - 1)
+
+    for k in range(parts):
+        pass_on(hid, r_h, 2, k)
+        pass_on(hid, r_h, 4, k)
+    gathered(ic, r_ic)
+    ict[...] = ic[...].astype(jnp.float32).T.astype(jnp.bfloat16)
+    for k in range(parts // 2):
+        pass_on(hid, r_h, 6, k)
+        pass_on(hid, r_h, 6, k + parts // 2)
+    for k in range(parts):
+        for index in (0, 2, 4, 6):
+            from_partner(hid, r_h, index, k)
+
+    def as_rows(row, ref, at):
+        for j in range(row.shape[1] // LANES):
+            ref[at + j : at + j + 1, :] = row[:, j * LANES : (j + 1) * LANES]
+
+    out_rows = 2 * chunk
+    written = []
+    zero_m = jnp.zeros((vec_m.shape[1], LANES), jnp.float32)
+    for slot in (0, 1):
+        vec_m[slot * n_mp] = zero_m
+    width_sum = jnp.zeros((1, cols), jnp.float32)
+    for k in range(parts):
+        rows = slice(k * out_rows, (k + 1) * out_rows)
+        grad = dot(hid[rows, :], oc[...], NN)
+        square = grad * grad + tiny_square
+        width_sum += jnp.sum(square, axis=0, keepdims=True)
+        lanes = sum(square[:, j * LANES : (j + 1) * LANES] for j in range(cols // LANES))
+        as_rows(jnp.sum(lanes.T, axis=0, keepdims=True), vec_d.at[0], k * out_rows // LANES)
+        go[rows, :] = grad.astype(jnp.bfloat16)
+        if k:
+            last = slice((k - 1) * out_rows, k * out_rows)
+            written.append(c.local(go.at[last], go_hbm.at[last]))
+        pass_on(pre, r_p, 2, k)
+        pass_on(pre, r_p, 4, k)
+    as_rows(width_sum, vec_m.at[0], 0)
+
+    def exchange_d(slot, height):
+        recv = c.take(n_dp)
+        src = vec_d.at[slot * n_dp, pl.ds(0, height)]
+        for index in range(1, n_dp):
+            dst = vec_d.at[slot * n_dp + index, pl.ds(0, height)]
+            c.remote(src, dst, recv + index, **on(index))
+
+        def total():
+            for index in range(1, n_dp):
+                c.arrived(vec_d.at[slot * n_dp + index, pl.ds(0, height)], recv + index, **on(index))
+            return sum(vec_d[slot * n_dp + index, :height] for index in range(n_dp))
+
+        return total
+
+    def exchange_m(slot):
+        recv = c.take(n_mp)
+        src = vec_m.at[slot * n_mp]
+        for index in range(1, n_mp):
+            device = dict(dp=d, mp=mp_of[index])
+            c.remote(src, vec_m.at[slot * n_mp + index], recv + index, **device)
+
+        def total():
+            for index in range(1, n_mp):
+                device = dict(dp=d, mp=mp_of[index])
+                c.arrived(vec_m.at[slot * n_mp + index], recv + index, **device)
+            return sum(vec_m[slot * n_mp + index] for index in range(n_mp))
+
+        return total
+
+    last = slice((parts - 1) * out_rows, parts * out_rows)
+    written.append(c.local(go.at[last], go_hbm.at[last]))
+    high = ff // LANES
+    hidden_out = exchange_d(0, high)
+    width_out = exchange_m(0)
+
+    racc[...] = jnp.zeros_like(racc)
+
+    def grad_in(which, k):
+        units = pl.ds(pl.multiple_of(which * half + k * chunk, chunk), chunk)
+        at = which * parts + k
+        grad = dot(ict[...], pre[:, units], NN)
+        square = grad * grad + tiny_square
+        as_rows(jnp.sum(square, axis=0, keepdims=True), vec_d.at[n_dp], at * chunk // LANES)
+        racc[...] += sum(square[:, j * LANES : (j + 1) * LANES] for j in range(chunk // LANES))
+        gi[at] = grad.astype(jnp.bfloat16)
+        return at, units
+
+    def write_in(at, units):
+        written.append(c.local(gi.at[at], gi_hbm.at[:, units]))
+
+    pending = []
+    for k in range(parts // 2):
+        ready = (k, k + parts // 2)
+        for j in ready:
+            pass_on(pre, r_p, 6, j)
+        if k == 0:
+            total = decay_rate * row_out[...] + (1.0 - decay_rate) * hidden_out() / width
+            rows_out = total
+            vec_m[2 * n_mp] = jnp.broadcast_to(jnp.sum(total), (8, LANES))
+            width_total = width_out()
+            fco_ref[...] = lax.rsqrt(decay_rate * col_out[...] + (1.0 - decay_rate) * width_total / (ff * n_mp))
+            for s in range(n_mp):
+                gone = jnp.logical_or(s != z, core != z // owned)
+
+                @pl.when(gone)
+                def _():
+                    c.arrived(rpb.at[s], r_rp + s, dp=chip * 2 + z // owned, mp=s)
+
+            @pl.when(core == z // owned)
+            def _():
+                rpb[z] = ipb[z - core * owned, mine, :]
+
+            ig_ref[...] = sum(rpb[s].astype(jnp.float32) for s in range(n_mp)).astype(jnp.bfloat16)
+        for j in ready:
+            for index in (2, 4, 6):
+                from_partner(pre, r_p, index, j)
+        if k == 0:
+            sum_rows = exchange_m(2)
+        for j in ready:
+            for which in (0, 1):
+                pending.append(grad_in(which, j))
+        if k:
+            for item in pending[:-4]:
+                write_in(*item)
+            pending = pending[-4:]
+    as_rows(jnp.sum(racc[...].T, axis=0, keepdims=True), vec_m.at[n_mp], 0)
+    for item in pending:
+        write_in(*item)
+    width_in = exchange_m(1)
+    hidden_in = exchange_d(1, high)
+    mean_out = sum_rows() / (ff * n_mp)
+    fro_ref[...] = step_size * lax.rsqrt(rows_out / mean_out[0:1, :])
+    rows_in = decay_rate * row_in[...] + (1.0 - decay_rate) * width_in() / (ff * n_mp)
+    vec_d[2 * n_dp, :8] = jnp.broadcast_to(jnp.sum(rows_in), (8, LANES))
+    fci_ref[...] = lax.rsqrt(decay_rate * col_in[...] + (1.0 - decay_rate) * hidden_in() / width)
+    mean_in = exchange_d(2, 8)() / width
+    fri_ref[...] = step_size * lax.rsqrt(rows_in / mean_in[0:1, :])
+    for which in range(owned):
+        for t in range(2):
+            copy, away = piece_copy(which, t)
+
+            @pl.when(away)
+            def _():
+                copy.wait_send()
+
+    c.drain()
+    for copy in written:
+        copy.wait()
+
+
+def fast_body(n_dp, n_mp, inputs, pre_act, out_grad, w_in, w_out, master_in, master_out, row_in, col_in, row_out, col_out):
+    tok, width = inputs.shape
+    ff = pre_act.shape[1]
+    cols = width // n_dp
+    parts = PARTS
+    chunk = ff // 2 // parts
+    in_rows = 2 * chunk
+    high, low = ff // LANES, cols // LANES
+    pad = (-low) % 8
+    as_tile = lambda v: jnp.pad(v.reshape(low, LANES), ((0, pad), (0, 0)))
+    slots = 3
+    bf, f32 = jnp.bfloat16, jnp.float32
+    anywhere = pl.BlockSpec(memory_space=pl.ANY)
+    vmem = pl.BlockSpec(memory_space=pltpu.VMEM)
+    shape = jax.ShapeDtypeStruct
+    plan = (n_dp, n_mp, tok, width, ff, cols, parts)
+    ig, go, gi, fro, fco, fri, fci = pl.pallas_call(
+        functools.partial(step_kernel, plan),
+        out_shape=(
+            shape((tok, width // n_mp), bf),
+            shape((ff, cols), bf),
+            shape((cols, ff), bf),
+            shape((high, LANES), f32),
+            shape((low + pad, LANES), f32),
+            shape((low + pad, LANES), f32),
+            shape((high, LANES), f32),
+        ),
+        in_specs=[anywhere] * 5 + [vmem] * 4,
+        out_specs=(vmem, anywhere, anywhere, vmem, vmem, vmem, vmem),
+        scratch_shapes=[
+            pltpu.VMEM((2 * tok, width), bf),
+            pltpu.VMEM((2 * tok, ff // 2), bf),
+            pltpu.VMEM((ff, n_dp * tok), bf),
+            pltpu.VMEM((n_dp * tok, ff), bf),
+            pltpu.VMEM((n_dp * tok, cols), bf),
+            pltpu.VMEM((n_dp * tok, cols), bf),
+            pltpu.VMEM((cols, n_dp * tok), bf),
+            pltpu.VMEM((slots, chunk, width), bf),
+            pltpu.VMEM((slots, in_rows, ff), bf),
+            pltpu.VMEM((n_mp // 2, 2 * tok, width // n_mp), bf),
+            pltpu.VMEM((n_mp, tok, width // n_mp), bf),
+            pltpu.VMEM((ff, cols), bf),
+            pltpu.VMEM((2 * parts, cols, chunk), bf),
+            pltpu.VMEM((cols, LANES), f32),
+            pltpu.VMEM((3 * n_dp, high, LANES), f32),
+            pltpu.VMEM((3 * n_mp, low + pad, LANES), f32),
+            pltpu.SemaphoreType.DMA((420,)),
+            pltpu.SemaphoreType.DMA((2 * slots,)),
+        ],
+        compiler_params=pltpu.CompilerParams(
+            collective_id=0, has_side_effects=True, vmem_limit_bytes=64 * 2**20 - 2**16
+        ),
+    )(
+        out_grad, pre_act, inputs, w_out, w_in,
+        row_out.reshape(high, LANES), as_tile(col_out), as_tile(row_in), col_in.reshape(high, LANES),
+    )
+    flat = lambda t, n: t.reshape(-1)[:n]
+    new_master_out = master_out - go.astype(f32) * flat(fro, ff)[:, None] * flat(fco, cols)[None, :]
+    new_master_in = master_in - gi.astype(f32) * flat(fri, cols)[:, None] * flat(fci, ff)[None, :]
+    return ig, new_master_in, new_master_out
+
+
+PARTS = 6
+
+
+def fits(mesh):
+    n_dp, n_mp = mesh.shape["dp"], mesh.shape["mp"]
+    return n_dp == 8 and n_mp == 4 and D % (n_dp * LANES) == 0 and FF % (n_mp * 2 * PARTS * LANES) == 0
 
 
 def solution(mesh):
@@ -100,4 +553,7 @@
         P("dp"),
     )
     out_specs = (P("dp", "mp"), P("dp", "mp"), P("mp", "dp"))
-    return jax.shard_map(body, mesh=mesh, in_specs=in_specs, out_specs=out_specs, check_vma=False)
+    run = body
+    if fits(mesh):
+        run = functools.partial(fast_body, mesh.shape["dp"], mesh.shape["mp"])
+    return jax.shard_map(run, mesh=mesh, in_specs=in_specs, out_specs=out_specs, check_vma=False)

time: 234 us -> 148 us (0.63)
  Pallas kernels: 0 us -> 123 us
  blocking collectives: 67.5 us -> 0 us
  matrix products: 62.1 us -> 0 us
  waiting for transfers between devices: 34.3 us -> 0 us
  between operations: 16.2 us -> 0.65 us
  starting transfers between devices: 14 us -> 0 us
  other arithmetic: 29.2 us -> 20.3 us
  local copies, waits for them, and re-layouts: 10.5 us -> 4.01 us
    pallas_call x0 -> x1, Pallas kernels: none -> 123 us  [fast_body(): pl.pallas_call(functools.partial(step_kernel, plan), out_shape=(shape((to...]
    psum x4 -> x0, blocking collectives: 67.5 us -> none  [the longest x1 23.4 us: body(): lax.psum((jnp.sum(square_out, axis=1), jnp.sum(width_out)), 'dp')]
    dot_general x4 -> x0, matrix products: 62.1 us -> none  [the longest x1 22.5 us: body(): lax.dot_general(out_grad, w_out, (((1,), (1,)), ((), ())), preferred_elem...]
    all_to_all x2 -> x0, waiting for transfers between devices: 34.2 us -> none  [the longest x1 19.7 us: body(): in_cols = lax.all_to_all(inputs, 'dp', 1, 0, tiled=True)]
    all_to_all x2 -> x0, starting transfers between devices: 9.5 us -> none  [the longest x1 5.2 us: body(): out_cols = lax.all_to_all(out_grad, 'dp', 1, 0, tiled=True)]
    ppermute x3 -> x0, starting transfers between devices: 4.43 us -> none  [scatter_pieces(): lax.ppermute(moved, axis, [(i, (i + shift) % size) for i in range(size)])]
    convert_element_type x2 -> x0, other arithmetic: 4.4 us -> none  [the longest x1 2.37 us: body(): hidden = active.astype(jnp.bfloat16)]
    all_to_all x2 -> x0, local copies, waits for them, and re-layouts: 4.31 us -> none  [the longest x1 2.6 us: body(): out_cols = lax.all_to_all(out_grad, 'dp', 1, 0, tiled=True)]
  transfers between devices with their start and end apart: 7 -> 0, of which waited for: 2 -> 0; matrix products, arithmetic and copies ran while one was open for 32% -> 0% of each run, Pallas kernels for 0% -> 0%
where the time goes in v1:
time: 148 us
  Pallas kernels  123 us (83%)
  other arithmetic  20.3 us (14%)
  local copies, waits for them, and re-layouts  4.01 us (3%)
    pallas_call x1, Pallas kernels, fast_body(): pl.pallas_call(functools.partial(step_kernel, plan), out_shape=(shape((to...  123 us
    sub x1, other arithmetic, fast_body(): master_out - go.astype(f32) * flat(fro, ff)[:, None] * flat(fco, cols)[No...  10.3 us
    sub x1, other arithmetic, fast_body(): master_in - gi.astype(f32) * flat(fri, cols)[:, None] * flat(fci, ff)[Non...  10 us

profile of v1, /device:TPU:0, one launch (start us, length us, event | category | flops | bytes accessed | tf_op | source)
XLA Modules:
  0.0 148.1 jit_solution(14513139707486154521)
XLA Ops:
  0.6 1.3 pad.8.row_in
  1.9 1.3 pad.7.col_out
  3.2 123.1 %shard_map.130 = (bf16[128,1536]{1,0:T(8,128)(2,1)}, bf16[3072,768]{1,0:T(8,128)(2,1)}, bf16[768,3072]{1,0:T(8,128)(2,1)}, f32[24,128]{1,0:T(8,128)}, f32[8,128]...) custom-call(bf16[128,6144]{1,0:T(8,128)(2,1)} %og_hbm.1, bf16[128,3072]{1,0:T(8,128)(2,1)} %pa_hbm.1, ...), custom_call_target="tpu_custom_call" | custom-call | tf_op jit(solution)/shard_map/pallas_call | solution.py:487
  126.3 0.7 slice_bitcast_fusion
  127.0 0.0 copy-start
  127.0 0.0 copy-start.2
  127.0 10.3 %multiply_subtract_fusion = f32[3072,768]{1,0:T(8,128)} fusion(f32[3072,768]{1,0:T(8,128)} %param.17, bf16[3072,768]{1,0:T(8,128)(2,1)} %get-tuple-element.14, f32[768]{0:T(1024)S(1)} %get-tuple-element.17, f32[3072]{0:T(1024)} %bitcast.13), kind=kLoop, calls=%fused_computation | loop fusion | flops 9437184 | bytes 23608320 | tf_op jit(solution)/shard_map/sub | solution.py:528
  137.3 0.0 copy-done
  137.3 0.0 copy-done.2
  137.3 0.0 copy-start.1
  137.3 10.0 %multiply_subtract_fusion.1 = f32[768,3072]{1,0:T(8,128)} fusion(f32[768,3072]{1,0:T(8,128)} %param.16, bf16[768,3072]{1,0:T(8,128)(2,1)S(1)} %copy-done, f32[3072]{0:T(1024)S(1)} %bitcast.12, f32[768]{0:T(1024)S(1)} %get-tuple-element.18), kind=kLoop, calls=%fused_computation.1 | loop fusion | flops 9437184 | bytes 23608320 | tf_op jit(solution)/shard_map/sub | solution.py:529
  147.4 0.0 copy-done.1
  147.4 0.7 copy.15
Async XLA Ops:
  127.0 10.3 %copy-start = (bf16[768,3072]{1,0:T(8,128)(2,1)S(1)}, bf16[768,3072]{1,0:T(8,128)(2,1)}, u32[]{:S(2)}) copy-start(bf16[768,3072]{1,0:T(8,128)(2,1)} %get-tuple-element.11) | copy-start | bytes 14155780
  127.0 10.3 %copy-start.2 = (f32[24,128]{1,0:T(8,128)S(1)}, f32[24,128]{1,0:T(8,128)}, u32[]{:S(2)}) copy-start(f32[24,128]{1,0:T(8,128)} %get-tuple-element.13) | copy-start | bytes 36868
  137.3 10.0 %copy-start.1 = (bf16[128,1536]{1,0:T(8,128)(2,1)S(1)}, bf16[128,1536]{1,0:T(8,128)(2,1)}, u32[]{:S(2)}) copy-start(bf16[128,1536]{1,0:T(8,128)(2,1)} %get-tuple-element.22) | copy-start | bytes 1179652

commit v2 on v0

--- a/solution.py
+++ b/solution.py
@@ -1,8 +1,11 @@
+import functools
 import math
 
 import jax
 import jax.numpy as jnp
 from jax import lax
+from jax.experimental import pallas as pl
+from jax.experimental.pallas import tpu as pltpu
 from jax.experimental.layout import Layout, with_layout_constraint
 from jax.sharding import PartitionSpec as P
 
@@ -83,6 +86,536 @@
     update_in = grad_in / jnp.sqrt(rows_in[:, None] * cols_in[None, :] / mean_in)
     new_master_in = master_in - step_size * update_in
     return (input_grad, new_master_in, new_master_out)
+
+
+MESH = pl.DeviceIdType.MESH
+NT = (((1,), (1,)), ((), ()))
+NN = (((1,), (0,)), ((), ()))
+LANES = 128
+
+
+def dot(left, right, dims):
+    return lax.dot_general(left, right, dims, preferred_element_type=jnp.float32)
+
+
+class Copies:
+    def __init__(self, sems, away):
+        self.sems = sems
+        self.away = away
+        self.count = 0
+        self.sent = []
+
+    def take(self, number=None):
+        first = self.count
+        self.count += number or 1
+        assert self.count <= SEMAPHORES
+        return first if number is None else range(first, self.count)
+
+    def local(self, src, dst, sem):
+        pltpu.make_async_copy(src, dst, self.sems.at[sem]).start()
+
+    def settled(self, region, sem):
+        pltpu.make_async_copy(region, region, self.sems.at[sem]).wait()
+
+    def sends(self, *regions):
+        sem = self.take()
+        self.sent += [(region, sem) for region in regions]
+        return sem
+
+    def moved(self, src, dst, send, recv, device):
+        return pltpu.make_async_remote_copy(
+            src_ref=src,
+            dst_ref=dst,
+            send_sem=self.sems.at[send],
+            recv_sem=self.sems.at[recv],
+            device_id=device,
+            device_id_type=MESH,
+        )
+
+    def remote(self, src, dst, send, recv, **device):
+        self.moved(src, dst, send, recv, device).start()
+
+    def arrived(self, region, recv):
+        self.moved(region, region, recv, recv, self.away).wait_recv()
+
+    def drain(self):
+        for region, sem in self.sent:
+            self.moved(region, region, sem, sem, self.away).wait_send()
+
+
+def step_kernel(
+    plan,
+    og_hbm, pa_hbm, in_hbm, wo_hbm, wi_hbm, ro_hbm, co_hbm, ri_hbm, ci_hbm,
+    ig_hbm, go, gi, fac,
+    og2, pa2, hid, pre, oc, ic, ict, wb, ipb, rpb, racc, vec_d, vec_m, igb,
+    row_out, col_out, row_in, col_in, sems,
+):
+    n_dp, n_mp, tok, width, ff, cols, parts = plan
+    half, depth = ff // 2, width // 2
+    piece = width // n_mp
+    chunk = half // parts
+    d, z = lax.axis_index("dp"), lax.axis_index("mp")
+    core, chip = lax.rem(d, 2), d // 2
+    base = pl.multiple_of(chip * 2 * tok, 2 * tok)
+    flip = lambda index: d + sum(
+        bit * (1 - 2 * lax.rem(d // bit, 2)) for bit in (1, 2, 4) if index & bit
+    )
+    turn = lambda index: z + sum(
+        bit * (1 - 2 * lax.rem(z // bit, 2)) for bit in (1, 2) if index & bit
+    )
+    dp_of = {index: flip(index) for index in range(1, n_dp)}
+    mp_of = {index: turn(index) for index in range(1, n_mp)}
+    on = lambda index: dict(dp=dp_of[index], mp=z)
+
+    barrier = pltpu.get_barrier_semaphore()
+    for index in range(1, n_dp):
+        pl.semaphore_signal(barrier, inc=1, device_id=on(index), device_id_type=MESH)
+    for index in range(1, n_mp):
+        for peer in (d, dp_of[1]):
+            device = dict(dp=peer, mp=mp_of[index])
+            pl.semaphore_signal(barrier, inc=1, device_id=device, device_id_type=MESH)
+
+    c = Copies(sems, on(1))
+    rows_of = lambda who: pl.ds(pl.multiple_of(who * tok, tok), tok)
+    mine = pl.ds(pl.multiple_of(core * tok, tok), tok)
+    other = pl.ds(pl.multiple_of((1 - core) * tok, tok), tok)
+    half_cols = lambda which: pl.ds(pl.multiple_of(which * half, half), half)
+    l_pa, l_og, l_oc, l_ic, l_ig = (c.take() for _ in range(5))
+    own_cols = pl.ds(pl.multiple_of(d * cols, cols), cols)
+    c.local(pa_hbm.at[:, half_cols(core)], pa2.at[mine], l_pa)
+    c.local(og_hbm, og2.at[mine], l_og)
+
+    side = width // ff
+    slots = wb.shape[0]
+    in_rows = side * chunk
+    n_out, n_in = half // chunk, depth // in_rows
+    w_sems = c.take(slots)[0]
+
+    def fetch(item):
+        slot = item % slots
+        if item < n_out:
+            rows = pl.ds(pl.multiple_of(core * half + item * chunk, chunk), chunk)
+            c.local(wo_hbm.at[rows], wb.at[slot], w_sems + slot)
+        elif item < n_out + n_in:
+            for part in range(side):
+                at = core * depth + (item - n_out) * in_rows + part * chunk
+                rows = pl.ds(pl.multiple_of(at, chunk), chunk)
+                to = wb.at[slot, :, pl.ds(part * ff, ff)]
+                c.local(wi_hbm.at[rows], to, w_sems + slot)
+
+    fetched = lambda item: c.settled(wb.at[item % slots], w_sems + item % slots)
+    for item in range(slots):
+        fetch(item)
+    c.local(og_hbm.at[:, own_cols], oc.at[rows_of(d)], l_oc)
+    c.local(in_hbm.at[:, own_cols], ic.at[rows_of(d)], l_ic)
+    vectors = ((ro_hbm, row_out), (co_hbm, col_out), (ri_hbm, row_in), (ci_hbm, col_in))
+    l_vectors = c.take(4)
+    for (src, dst), sem in zip(vectors, l_vectors):
+        c.local(src, dst, sem)
+
+    pl.semaphore_wait(barrier, n_dp - 1 + 2 * (n_mp - 1))
+
+    even = lax.rem(z, 2)
+    part_rows = lambda who, which: pl.ds(
+        pl.multiple_of(who * tok + which * (tok // 2), tok // 2), tok // 2
+    )
+    beside = dict(dp=d, mp=mp_of[1])
+
+    def spread(src, dst):
+        near, beyond, partner = c.take(3)
+        send = c.sends(dst.at[pl.ds(0, (n_dp - 1) * tok)])
+        for index in (2, 4, 6, 3, 5, 7):
+            their = pl.ds(pl.multiple_of(dp_of[index] * cols, cols), cols)
+            c.remote(src.at[part_rows(0, even), their], dst.at[part_rows(d, even)], send, near, **on(index))
+        their = pl.ds(pl.multiple_of(dp_of[1] * cols, cols), cols)
+        c.remote(src.at[:, their], dst.at[rows_of(d)], send, partner, **on(1))
+
+        def hand_on():
+            c.arrived(dst.at[pl.ds(0, (n_dp - 2) * (tok // 2))], near)
+            for index in range(2, n_dp):
+                rows = dst.at[part_rows(dp_of[index], even)]
+                c.remote(rows, rows, send, beyond, **beside)
+
+        def gathered():
+            c.arrived(dst.at[rows_of(dp_of[1])], partner)
+            c.arrived(dst.at[pl.ds(0, (n_dp - 2) * (tok // 2))], beyond)
+
+        return hand_on, gathered
+
+    hand_on_oc, gathered_oc = spread(og_hbm, oc)
+    r_pa, r_og = c.take(2)
+    c.remote(
+        pa_hbm.at[:, half_cols(1 - core)], pa2.at[mine], c.sends(pa2.at[mine]), r_pa, **on(1)
+    )
+    c.remote(og_hbm, og2.at[mine], c.sends(og2.at[mine]), r_og, **on(1))
+    hand_on_ic, gathered_ic = spread(in_hbm, ic)
+
+    def block(dst, index, which, k):
+        tokens = pl.ds(pl.multiple_of((dp_of[index] if index else d) // 2 * 2 * tok, 2 * tok), 2 * tok)
+        units = pl.ds(pl.multiple_of(which * half + k * chunk, chunk), chunk)
+        return dst.at[units, tokens] if dst is hid else dst.at[tokens, units]
+
+    class Stream:
+        def __init__(self, dst):
+            self.dst = dst
+            self.near = {index: c.take(parts) for index in (2, 4, 6)}
+            self.pairs = {index: c.take() for index in (0, 2, 4)}
+            self.pairs[6] = c.take(parts)
+            units, tokens = pl.ds(0, parts // 2 * 3 * chunk), pl.ds(0, 2 * tok)
+            some = dst.at[units, tokens] if dst is hid else dst.at[tokens, units]
+            whole = pl.ds(0, n_dp // 2 * tok)
+            most = dst.at[:, whole] if dst is hid else dst.at[whole, :]
+            self.send = {2: c.sends(some), 4: c.sends(some), 1: c.sends(most)}
+
+        def across(self, index, k):
+            return self.pairs[6][k] if index == 6 else self.pairs[index]
+
+        def own(self, k, index):
+            src = block(self.dst, 0, core, k)
+            recv = self.pairs[0] if index == 1 else self.near[index][k]
+            c.remote(src, src, self.send[index], recv, **on(index))
+
+        def pass_on(self, index, k):
+            src = block(self.dst, index, core, k)
+            c.arrived(src, self.near[index][k])
+            if index == 2 and k < parts // 2:
+                c.remote(src, src, self.send[4], self.near[6][k], **on(4))
+            if index == 4 and k >= parts // 2:
+                c.remote(src, src, self.send[2], self.near[6][k], **on(2))
+            c.remote(src, src, self.send[1], self.across(index, k), **on(1))
+
+        def whole_from_partner(self, index):
+            tokens = pl.ds(pl.multiple_of((dp_of[index] if index else d) // 2 * 2 * tok, 2 * tok), 2 * tok)
+            units = half_cols(1 - core)
+            region = self.dst.at[units, tokens] if self.dst is hid else self.dst.at[tokens, units]
+            c.arrived(region, self.pairs[index])
+
+        def diagonal_from_partner(self, k):
+            c.arrived(block(self.dst, 6, 1 - core, k), self.pairs[6][k])
+
+    h_flow, p_flow = Stream(hid), Stream(pre)
+    c.settled(pa2.at[mine], l_pa)
+    c.arrived(pa2.at[other], r_pa)
+
+    for k in range(parts):
+        units = slice(k * chunk, (k + 1) * chunk)
+        active, _ = gelu_parts(pa2[:, units].astype(jnp.float32))
+        target = pl.ds(pl.multiple_of(core * half + k * chunk, chunk), chunk)
+        hid[target, pl.ds(base, 2 * tok)] = active.T.astype(jnp.bfloat16)
+        if k:
+            for index in (2, 4, 1):
+                h_flow.own(k - 1, index)
+    c.settled(og2.at[mine], l_og)
+    c.arrived(og2.at[other], r_og)
+    for k in range(parts):
+        fetched(k)
+        hid_grad = dot(og2[...], wb[k % slots], NT)
+        _, slope = gelu_parts(pa2[:, k * chunk : (k + 1) * chunk].astype(jnp.float32))
+        target = pl.ds(pl.multiple_of(core * half + k * chunk, chunk), chunk)
+        pre[pl.ds(base, 2 * tok), target] = (hid_grad * slope).astype(jnp.bfloat16)
+        fetch(k + slots)
+        if k:
+            p_flow.own(k - 1, 1)
+        else:
+            for index in (2, 4, 1):
+                h_flow.own(parts - 1, index)
+    hand_on_oc()
+    p_flow.own(parts - 1, 1)
+    p_flow.whole_from_partner(0)
+
+    r_rp = c.take(n_mp)[0]
+    owned = n_mp // 2
+    s_rp = c.take(owned * 2)[0]
+
+    def piece_copy(which, t):
+        to = core * owned + which
+        return pltpu.make_async_remote_copy(
+            src_ref=ipb.at[which, pl.ds(t * tok, tok)],
+            dst_ref=rpb.at[z],
+            send_sem=sems.at[s_rp + which * 2 + t],
+            recv_sem=sems.at[r_rp + z],
+            device_id=dict(dp=chip * 2 + t, mp=to),
+            device_id_type=MESH,
+        ), jnp.logical_or(to != z, core != t)
+
+    def send_pieces(which):
+        for t in range(2):
+            copy, away = piece_copy(which, t)
+
+            @pl.when(away)
+            def _():
+                copy.start()
+
+    per = n_in // owned
+    for k in range(n_in):
+        item = n_out + k
+        fetched(item)
+        for part in range(side):
+            rows = wb[item % slots, :, part * ff : (part + 1) * ff]
+            value = dot(pre[pl.ds(base, 2 * tok), :], rows, NT).astype(jnp.bfloat16)
+            at = k % per * in_rows + part * chunk
+            ipb[k // per, :, at : at + chunk] = value
+        fetch(item + slots)
+    hand_on_ic()
+    for which in range(owned):
+        send_pieces(which)
+
+    for k in range(parts):
+        h_flow.pass_on(2, k)
+        h_flow.pass_on(4, k)
+        if k == parts // 2 - 1:
+            for j in range(parts):
+                p_flow.own(j, 4)
+    for k in range(parts):
+        p_flow.own(k, 2)
+    for (_, dst), sem in zip(vectors, l_vectors):
+        c.settled(dst, sem)
+    c.settled(oc.at[rows_of(d)], l_oc)
+    c.settled(ic.at[rows_of(d)], l_ic)
+    for k in range(parts // 2):
+        h_flow.pass_on(6, k)
+        h_flow.pass_on(6, k + parts // 2)
+    gathered_ic()
+    ict[...] = ic[...].astype(jnp.float32).T.astype(jnp.bfloat16)
+    gathered_oc()
+    for index in (0, 2, 4):
+        h_flow.whole_from_partner(index)
+    for k in range(parts):
+        h_flow.diagonal_from_partner(k)
+
+    def as_rows(row, ref, at):
+        for j in range(row.shape[1] // LANES):
+            ref[pl.ds(at + j, 1), :] = row[:, j * LANES : (j + 1) * LANES]
+
+    out_rows = 2 * chunk
+    fac[...] = jnp.zeros_like(fac)
+    zero_m = jnp.zeros((vec_m.shape[1], LANES), jnp.float32)
+    for slot in (0, 1):
+        vec_m[slot * n_mp] = zero_m
+    width_sum = jnp.zeros((1, cols), jnp.float32)
+    for k in range(parts):
+        rows = slice(k * out_rows, (k + 1) * out_rows)
+        grad = dot(hid[rows, :], oc[...], NN)
+        square = grad * grad + tiny_square
+        width_sum += jnp.sum(square, axis=0, keepdims=True)
+        lanes = sum(square[:, j * LANES : (j + 1) * LANES] for j in range(cols // LANES))
+        as_rows(jnp.sum(lanes.T, axis=0, keepdims=True), vec_d.at[0], k * out_rows // LANES)
+        go[rows, :] = grad.astype(jnp.bfloat16)
+        p_flow.pass_on(2, k)
+        p_flow.pass_on(4, k)
+    as_rows(width_sum, vec_m.at[0], 0)
+
+    def exchange(table, slot, peers, height):
+        recv = c.take()
+        first = slot * (len(peers) + 1)
+        rows = pl.ds(0, height)
+        there = table.at[pl.ds(first + 1, len(peers)), rows]
+        send = c.sends(there)
+        for at, device in enumerate(peers):
+            c.remote(table.at[first, rows], table.at[first + 1 + at, rows], send, recv, **device)
+
+        def total():
+            c.arrived(there, recv)
+            return sum(table[first + at, :height] for at in range(len(peers) + 1))
+
+        return total
+
+    dp_peers = [on(index) for index in range(1, n_dp)]
+    mp_peers = [dict(dp=d, mp=mp_of[index]) for index in range(1, n_mp)]
+    exchange_d = lambda slot, height: exchange(vec_d, slot, dp_peers, height)
+    exchange_m = lambda slot: exchange(vec_m, slot, mp_peers, vec_m.shape[1])
+    high = ff // LANES
+    hidden_out = exchange_d(0, high)
+    width_out = exchange_m(0)
+
+    racc[...] = jnp.zeros_like(racc)
+
+    def grad_in(which, k):
+        units = pl.ds(pl.multiple_of(which * half + k * chunk, chunk), chunk)
+        at = which * parts + k
+        grad = dot(ict[...], pre[:, units], NN)
+        square = grad * grad + tiny_square
+        as_rows(jnp.sum(square, axis=0, keepdims=True), vec_d.at[n_dp], at * chunk // LANES)
+        racc[...] += sum(square[:, j * LANES : (j + 1) * LANES] for j in range(chunk // LANES))
+        gi[:, units] = grad.astype(jnp.bfloat16)
+
+    for index in (2, 4):
+        p_flow.whole_from_partner(index)
+    for k in range(parts // 2):
+        ready = (k, k + parts // 2)
+        for j in ready:
+            p_flow.pass_on(6, j)
+        for j in ready:
+            grad_in(core, j)
+        for j in ready:
+            p_flow.diagonal_from_partner(j)
+        for j in ready:
+            grad_in(1 - core, j)
+    as_rows(jnp.sum(racc[...].T, axis=0, keepdims=True), vec_m.at[n_mp], 0)
+    width_in = exchange_m(1)
+    hidden_in = exchange_d(1, high)
+    low = cols // LANES
+    rows_out = decay_rate * row_out[...] + (1.0 - decay_rate) * hidden_out() / width
+    vec_m[2 * n_mp] = jnp.broadcast_to(jnp.sum(rows_out), vec_m.shape[1:])
+    cols_out = decay_rate * col_out[...] + (1.0 - decay_rate) * width_out()[:low] / (ff * n_mp)
+    for s in range(n_mp):
+        gone = jnp.logical_or(s != z, core != z // owned)
+
+        @pl.when(gone)
+        def _():
+            c.arrived(rpb.at[s], r_rp + s)
+
+    sum_rows = exchange_m(2)
+
+    @pl.when(core == z // owned)
+    def _():
+        rpb[z] = ipb[z - core * owned, mine, :]
+
+    rows_in = decay_rate * row_in[...] + (1.0 - decay_rate) * width_in()[:low] / (ff * n_mp)
+    vec_d[2 * n_dp, :8] = jnp.broadcast_to(jnp.sum(rows_in), (8, LANES))
+    igb[...] = sum(rpb[s].astype(jnp.float32) for s in range(n_mp)).astype(jnp.bfloat16)
+    sum_rows_in = exchange_d(2, 8)
+    c.local(igb, ig_hbm, l_ig)
+    fac[high : 2 * high] = lax.rsqrt(
+        decay_rate * col_in[...] + (1.0 - decay_rate) * hidden_in() / width
+    )
+    fac[2 * high : 2 * high + low] = lax.rsqrt(cols_out)
+    mean_out = sum_rows() / (ff * n_mp)
+    fac[:high] = step_size * lax.rsqrt(rows_out / mean_out[0:1, :])
+    mean_in = sum_rows_in() / width
+    fac[2 * high + 8 : 2 * high + 8 + low] = step_size * lax.rsqrt(rows_in / mean_in[0:1, :])
+    c.settled(igb, l_ig)
+    for which in range(owned):
+        for t in range(2):
+            copy, away = piece_copy(which, t)
+
+            @pl.when(away)
+            def _():
+                copy.wait_send()
+
+    c.drain()
+
+
+def update_kernel(plan, mo, mi_hbm, go, gi, fac, new_out, new_in, out_b, in_b, sems):
+    ff, cols, tiles = plan
+    high, low = ff // LANES, cols // LANES
+    work = []
+    for new, old, stage, grad, first, height, across, rows_at, cols_at in (
+        (new_out, mo, out_b, go, 0, high, low, 0, 2 * high),
+        (new_in, in_b, in_b, gi, tiles, low, high, 2 * high + 8, high),
+    ):
+        for tile in range(tiles):
+            bands = range(tile * height // tiles, (tile + 1) * height // tiles)
+            rows = slice(bands[0] * LANES, (bands[-1] + 1) * LANES)
+            fetch = None
+            if old is stage:
+                fetch = pltpu.make_async_copy(mi_hbm.at[rows], stage.at[rows], sems.at[0, tile])
+                fetch.start()
+            store = pltpu.make_async_copy(stage.at[rows], new.at[rows], sems.at[1, first + tile])
+            work.append((fetch, store, old, stage, grad, bands, across, rows_at, cols_at))
+    turned = fac[...].T
+    for fetch, store, old, stage, grad, bands, across, rows_at, cols_at in work:
+        if fetch is not None:
+            fetch.wait()
+        for band in bands:
+            rows = slice(band * LANES, (band + 1) * LANES)
+            down = jnp.broadcast_to(turned[:, rows_at + band : rows_at + band + 1], (LANES, LANES))
+
+            def lane_group(j, carry):
+                at = pl.ds(pl.multiple_of(j * LANES, LANES), LANES)
+                scale = down * fac[pl.ds(cols_at + j, 1), :]
+                stage[rows, at] = old[rows, at] - grad[rows, at].astype(jnp.float32) * scale
+                return carry
+
+            lax.fori_loop(0, across, lane_group, 0, unroll=6)
+        store.start()
+    for _, store, *_ in work:
+        store.wait()
+
+
+def fast_body(n_dp, n_mp, inputs, pre_act, out_grad, w_in, w_out, master_in, master_out, row_in, col_in, row_out, col_out):
+    tok, width = inputs.shape
+    ff = pre_act.shape[1]
+    cols = width // n_dp
+    parts = PARTS
+    chunk = ff // 2 // parts
+    high, low = ff // LANES, cols // LANES
+    slots, tiles = 2, math.gcd(high, low)
+    bf, f32 = jnp.bfloat16, jnp.float32
+    anywhere = pl.BlockSpec(memory_space=pl.ANY)
+    vmem = pl.BlockSpec(memory_space=pltpu.VMEM)
+    shape = jax.ShapeDtypeStruct
+    plan = (n_dp, n_mp, tok, width, ff, cols, parts)
+    in_hbm = lambda array: pltpu.with_memory_space_constraint(array, pltpu.HBM)
+    in_vmem = lambda array: pltpu.with_memory_space_constraint(array, pltpu.VMEM)
+    ig, *held = pl.pallas_call(
+        functools.partial(step_kernel, plan),
+        out_shape=(
+            shape((tok, width // n_mp), bf),
+            pltpu.VMEM((ff, cols), bf),
+            pltpu.VMEM((cols, ff), bf),
+            pltpu.VMEM((2 * high + 16, LANES), f32),
+        ),
+        in_specs=[anywhere] * 9,
+        out_specs=(anywhere,) + (vmem,) * 3,
+        scratch_shapes=[
+            pltpu.VMEM((2 * tok, width), bf),
+            pltpu.VMEM((2 * tok, ff // 2), bf),
+            pltpu.VMEM((ff, n_dp * tok), bf),
+            pltpu.VMEM((n_dp * tok, ff), bf),
+            pltpu.VMEM((n_dp * tok, cols), bf),
+            pltpu.VMEM((n_dp * tok, cols), bf),
+            pltpu.VMEM((cols, n_dp * tok), bf),
+            pltpu.VMEM((slots, chunk, width), bf),
+            pltpu.VMEM((n_mp // 2, 2 * tok, width // n_mp), bf),
+            pltpu.VMEM((n_mp, tok, width // n_mp), bf),
+            pltpu.VMEM((cols, LANES), f32),
+            pltpu.VMEM((3 * n_dp, high, LANES), f32),
+            pltpu.VMEM((3 * n_mp, 8, LANES), f32),
+            pltpu.VMEM((tok, width // n_mp), bf),
+            pltpu.VMEM((high, LANES), f32),
+            pltpu.VMEM((low, LANES), f32),
+            pltpu.VMEM((low, LANES), f32),
+            pltpu.VMEM((high, LANES), f32),
+            pltpu.SemaphoreType.DMA((SEMAPHORES,)),
+        ],
+        compiler_params=pltpu.CompilerParams(
+            collective_id=0, has_side_effects=True, vmem_limit_bytes=K1_VMEM
+        ),
+    )(
+        *map(
+            in_hbm,
+            (
+                out_grad, pre_act, inputs, w_out, w_in,
+                row_out.reshape(high, LANES), col_out.reshape(low, LANES),
+                row_in.reshape(low, LANES), col_in.reshape(high, LANES),
+            ),
+        )
+    )
+    new_master_out, new_master_in = pl.pallas_call(
+        functools.partial(update_kernel, (ff, cols, tiles)),
+        out_shape=(shape((ff, cols), f32), shape((cols, ff), f32)),
+        in_specs=[vmem, anywhere, vmem, vmem, vmem],
+        out_specs=(anywhere,) * 2,
+        scratch_shapes=[
+            pltpu.VMEM((ff, cols), f32),
+            pltpu.VMEM((cols, ff), f32),
+            pltpu.SemaphoreType.DMA((2, 2 * tiles)),
+        ],
+        compiler_params=pltpu.CompilerParams(vmem_limit_bytes=K2_VMEM),
+    )(in_vmem(master_out), in_hbm(master_in), *map(in_vmem, held))
+    return ig, new_master_in, new_master_out
+
+
+SEMAPHORES = 110
+K1_VMEM = 34 * 2**20
+K2_VMEM = 21 * 2**20
+PARTS = 6
+
+
+def fits(mesh):
+    n_dp, n_mp = mesh.shape["dp"], mesh.shape["mp"]
+    return n_dp == 8 and n_mp == 4 and D % (n_dp * LANES) == 0 and D <= 8 * n_dp * LANES and D * n_mp % FF == 0 and FF % (n_mp * 2 * PARTS * LANES) == 0
 
 
 def solution(mesh):
@@ -100,4 +633,7 @@
         P("dp"),
     )
     out_specs = (P("dp", "mp"), P("dp", "mp"), P("mp", "dp"))
-    return jax.shard_map(body, mesh=mesh, in_specs=in_specs, out_specs=out_specs, check_vma=False)
+    run = body
+    if fits(mesh):
+        run = functools.partial(fast_body, mesh.shape["dp"], mesh.shape["mp"])
+    return jax.shard_map(run, mesh=mesh, in_specs=in_specs, out_specs=out_specs, check_vma=False)

time: 234 us -> 101 us (0.43)
  Pallas kernels: 0 us -> 99 us
  blocking collectives: 67.5 us -> 0 us
  matrix products: 62.1 us -> 0 us
  waiting for transfers between devices: 34.3 us -> 0 us
  other arithmetic: 29.2 us -> 0 us
  between operations: 16.2 us -> 0.67 us
  starting transfers between devices: 14 us -> 0 us
  local copies, waits for them, and re-layouts: 10.5 us -> 0.75 us
    pallas_call x0 -> x2, Pallas kernels: none -> 99 us  [the longest x1 88 us: fast_body(): pl.pallas_call(functools.partial(step_kernel, plan), out_shape=(shape((to...]
    psum x4 -> x0, blocking collectives: 67.5 us -> none  [the longest x1 23.4 us: body(): lax.psum((jnp.sum(square_out, axis=1), jnp.sum(width_out)), 'dp')]
    dot_general x4 -> x0, matrix products: 62.1 us -> none  [the longest x1 22.5 us: body(): lax.dot_general(out_grad, w_out, (((1,), (1,)), ((), ())), preferred_elem...]
    all_to_all x2 -> x0, waiting for transfers between devices: 34.2 us -> none  [the longest x1 19.7 us: body(): in_cols = lax.all_to_all(inputs, 'dp', 1, 0, tiled=True)]
    sub x2 -> x0, other arithmetic: 23 us -> none  [the longest x1 11.7 us: body(): new_master_in = master_in - step_size * update_in]
    all_to_all x2 -> x0, starting transfers between devices: 9.5 us -> none  [the longest x1 5.2 us: body(): out_cols = lax.all_to_all(out_grad, 'dp', 1, 0, tiled=True)]
    ppermute x3 -> x0, starting transfers between devices: 4.43 us -> none  [scatter_pieces(): lax.ppermute(moved, axis, [(i, (i + shift) % size) for i in range(size)])]
    convert_element_type x2 -> x0, other arithmetic: 4.4 us -> none  [the longest x1 2.37 us: body(): hidden = active.astype(jnp.bfloat16)]
  transfers between devices with their start and end apart: 7 -> 0, of which waited for: 2 -> 0; matrix products, arithmetic and copies ran while one was open for 32% -> 0% of each run, Pallas kernels for 0% -> 0%
where the time goes in v2:
time: 101 us; the launch traced here: 100 us
  Pallas kernels  99 us (98%)
    pallas_call x1, Pallas kernels, fast_body(): pl.pallas_call(functools.partial(step_kernel, plan), out_shape=(shape((to...  88 us
    pallas_call x1, Pallas kernels, fast_body(): pl.pallas_call(functools.partial(update_kernel, (ff, cols, tiles)), out_s...  11 us

profile of v2, /device:TPU:0, one launch (start us, length us, event | category | flops | bytes accessed | tf_op | source)
XLA Modules:
  0.0 100.4 jit_solution(1394290226290224371)
XLA Ops:
  0.6 0.0 copy-start
  0.6 88.0 %shard_map.130 = (bf16[128,1536]{1,0:T(8,128)(2,1)S(1)}, bf16[3072,768]{1,0:T(8,128)(2,1)S(1)}, bf16[768,3072]{1,0:T(8,128)(2,1)S(1)}, f32[64,128]{1,0:T(8,128)S(1)}) custom-call(bf16[128,6144]{1,0:T(8,128)(2,1)} %og_hbm.1, bf16[128,3072]{1,0:T(8,128)(2,1)} %pa_hbm.1, bf16[128,6144]{1,0:T(8,128)(2,1)} %in_hbm.1, bf16[3072,6144]{1,0:T(8,128)(2,1)} %wo_hbm.1, ...), custom_call_target="tpu_custom_call" | custom-call | tf_op jit(solution)/shard_map/pallas_call | solution.py:551
  88.7 0.0 copy-done
  88.7 11.0 %shard_map.131 = (f32[3072,768]{1,0:T(8,128)}, f32[768,3072]{1,0:T(8,128)}) custom-call(f32[3072,768]{1,0:T(8,128)S(1)} %copy-done, f32[768,3072]{1,0:T(8,128)} %mi_hbm.1, bf16[3072,768]{1,0:T(8,128)(2,1)S(1)} %get-tuple-element.10.go, bf16[768,3072]{1,0:T(8,128)(2,1)S(1)} %get-tuple-element.11.gi, f32[64,128]{1,0:T(8,128)S(1)} %get-tuple-element.12.fac), custom_call_target="tpu_custom_call" | custom-call | tf_op jit(solution)/shard_map/pallas_call | solution.py:595
  99.7 0.7 copy.15
Async XLA Ops:
  0.6 88.0 %copy-start = (f32[3072,768]{1,0:T(8,128)S(1)}, f32[3072,768]{1,0:T(8,128)}, u32[]{:S(2)}) copy-start(f32[3072,768]{1,0:T(8,128)} %mo.1) | copy-start | bytes 28311556

commit v3 on v2

--- a/solution.py
+++ b/solution.py
@@ -146,8 +146,8 @@
 def step_kernel(
     plan,
     og_hbm, pa_hbm, in_hbm, wo_hbm, wi_hbm, ro_hbm, co_hbm, ri_hbm, ci_hbm,
-    ig_hbm, go, gi, fac,
-    og2, pa2, hid, pre, oc, ic, ict, wb, ipb, rpb, racc, vec_d, vec_m, igb,
+    go, gi, fac, igb,
+    og2, pa2, hid, pre, oc, ic, ict, wb, rpb, racc, vec_d, vec_m,
     row_out, col_out, row_in, col_in, sems,
 ):
     n_dp, n_mp, tok, width, ff, cols, parts = plan
@@ -180,7 +180,7 @@
     mine = pl.ds(pl.multiple_of(core * tok, tok), tok)
     other = pl.ds(pl.multiple_of((1 - core) * tok, tok), tok)
     half_cols = lambda which: pl.ds(pl.multiple_of(which * half, half), half)
-    l_pa, l_og, l_oc, l_ic, l_ig = (c.take() for _ in range(5))
+    l_pa, l_og, l_oc, l_ic = (c.take() for _ in range(4))
     own_cols = pl.ds(pl.multiple_of(d * cols, cols), cols)
     c.local(pa_hbm.at[:, half_cols(core)], pa2.at[mine], l_pa)
     c.local(og_hbm, og2.at[mine], l_og)
@@ -330,7 +330,7 @@
     def piece_copy(which, t):
         to = core * owned + which
         return pltpu.make_async_remote_copy(
-            src_ref=ipb.at[which, pl.ds(t * tok, tok)],
+            src_ref=og2.at[pl.ds(t * tok, tok), pl.ds(which * piece, piece)],
             dst_ref=rpb.at[z],
             send_sem=sems.at[s_rp + which * 2 + t],
             recv_sem=sems.at[r_rp + z],
@@ -346,19 +346,16 @@
             def _():
                 copy.start()
 
-    per = n_in // owned
     for k in range(n_in):
         item = n_out + k
         fetched(item)
         for part in range(side):
             rows = wb[item % slots, :, part * ff : (part + 1) * ff]
             value = dot(pre[pl.ds(base, 2 * tok), :], rows, NT).astype(jnp.bfloat16)
-            at = k % per * in_rows + part * chunk
-            ipb[k // per, :, at : at + chunk] = value
+            at = k * in_rows + part * chunk
+            og2[:, at : at + chunk] = value
         fetch(item + slots)
     hand_on_ic()
-    for which in range(owned):
-        send_pieces(which)
 
     for k in range(parts):
         h_flow.pass_on(2, k)
@@ -366,6 +363,8 @@
         if k == parts // 2 - 1:
             for j in range(parts):
                 p_flow.own(j, 4)
+        if k >= parts - owned:
+            send_pieces(k - parts + owned)
     for k in range(parts):
         p_flow.own(k, 2)
     for (_, dst), sem in zip(vectors, l_vectors):
@@ -375,8 +374,6 @@
     for k in range(parts // 2):
         h_flow.pass_on(6, k)
         h_flow.pass_on(6, k + parts // 2)
-    gathered_ic()
-    ict[...] = ic[...].astype(jnp.float32).T.astype(jnp.bfloat16)
     gathered_oc()
     for index in (0, 2, 4):
         h_flow.whole_from_partner(index)
@@ -403,6 +400,8 @@
         go[rows, :] = grad.astype(jnp.bfloat16)
         p_flow.pass_on(2, k)
         p_flow.pass_on(4, k)
+    gathered_ic()
+    ict[...] = ic[...].astype(jnp.float32).T.astype(jnp.bfloat16)
     as_rows(width_sum, vec_m.at[0], 0)
 
     def exchange(table, slot, peers, height):
@@ -469,13 +468,13 @@
 
     @pl.when(core == z // owned)
     def _():
-        rpb[z] = ipb[z - core * owned, mine, :]
+        there = pl.ds(pl.multiple_of((z - core * owned) * piece, piece), piece)
+        rpb[z] = og2[mine, there]
 
     rows_in = decay_rate * row_in[...] + (1.0 - decay_rate) * width_in()[:low] / (ff * n_mp)
     vec_d[2 * n_dp, :8] = jnp.broadcast_to(jnp.sum(rows_in), (8, LANES))
     igb[...] = sum(rpb[s].astype(jnp.float32) for s in range(n_mp)).astype(jnp.bfloat16)
     sum_rows_in = exchange_d(2, 8)
-    c.local(igb, ig_hbm, l_ig)
     fac[high : 2 * high] = lax.rsqrt(
         decay_rate * col_in[...] + (1.0 - decay_rate) * hidden_in() / width
     )
@@ -484,7 +483,6 @@
     fac[:high] = step_size * lax.rsqrt(rows_out / mean_out[0:1, :])
     mean_in = sum_rows_in() / width
     fac[2 * high + 8 : 2 * high + 8 + low] = step_size * lax.rsqrt(rows_in / mean_in[0:1, :])
-    c.settled(igb, l_ig)
     for which in range(owned):
         for t in range(2):
             copy, away = piece_copy(which, t)
@@ -496,40 +494,33 @@
     c.drain()
 
 
-def update_kernel(plan, mo, mi_hbm, go, gi, fac, new_out, new_in, out_b, in_b, sems):
+def update_kernel(plan, mo, mi, go, gi, fac, ig, new_ig, new_out, new_in, out_b, in_b, sems):
     ff, cols, tiles = plan
     high, low = ff // LANES, cols // LANES
-    work = []
+    stores = [pltpu.make_async_copy(ig, new_ig, sems.at[2 * tiles])]
+    stores[0].start()
+    turned = fac[...].T
     for new, old, stage, grad, first, height, across, rows_at, cols_at in (
         (new_out, mo, out_b, go, 0, high, low, 0, 2 * high),
-        (new_in, in_b, in_b, gi, tiles, low, high, 2 * high + 8, high),
+        (new_in, mi, in_b, gi, tiles, low, high, 2 * high + 8, high),
     ):
         for tile in range(tiles):
             bands = range(tile * height // tiles, (tile + 1) * height // tiles)
+            for band in bands:
+                rows = slice(band * LANES, (band + 1) * LANES)
+                down = jnp.broadcast_to(turned[:, rows_at + band : rows_at + band + 1], (LANES, LANES))
+
+                def lane_group(j, carry):
+                    at = pl.ds(pl.multiple_of(j * LANES, LANES), LANES)
+                    scale = down * fac[pl.ds(cols_at + j, 1), :]
+                    stage[rows, at] = old[rows, at] - grad[rows, at].astype(jnp.float32) * scale
+                    return carry
+
+                lax.fori_loop(0, across, lane_group, 0, unroll=3)
             rows = slice(bands[0] * LANES, (bands[-1] + 1) * LANES)
-            fetch = None
-            if old is stage:
-                fetch = pltpu.make_async_copy(mi_hbm.at[rows], stage.at[rows], sems.at[0, tile])
-                fetch.start()
-            store = pltpu.make_async_copy(stage.at[rows], new.at[rows], sems.at[1, first + tile])
-            work.append((fetch, store, old, stage, grad, bands, across, rows_at, cols_at))
-    turned = fac[...].T
-    for fetch, store, old, stage, grad, bands, across, rows_at, cols_at in work:
-        if fetch is not None:
-            fetch.wait()
-        for band in bands:
-            rows = slice(band * LANES, (band + 1) * LANES)
-            down = jnp.broadcast_to(turned[:, rows_at + band : rows_at + band + 1], (LANES, LANES))
-
-            def lane_group(j, carry):
-                at = pl.ds(pl.multiple_of(j * LANES, LANES), LANES)
-                scale = down * fac[pl.ds(cols_at + j, 1), :]
-                stage[rows, at] = old[rows, at] - grad[rows, at].astype(jnp.float32) * scale
-                return carry
-
-            lax.fori_loop(0, across, lane_group, 0, unroll=6)
-        store.start()
-    for _, store, *_ in work:
+            stores.append(pltpu.make_async_copy(stage.at[rows], new.at[rows], sems.at[first + tile]))
+            stores[-1].start()
+    for store in stores:
         store.wait()
 
 
@@ -548,16 +539,16 @@
     plan = (n_dp, n_mp, tok, width, ff, cols, parts)
     in_hbm = lambda array: pltpu.with_memory_space_constraint(array, pltpu.HBM)
     in_vmem = lambda array: pltpu.with_memory_space_constraint(array, pltpu.VMEM)
-    ig, *held = pl.pallas_call(
+    held = pl.pallas_call(
         functools.partial(step_kernel, plan),
         out_shape=(
-            shape((tok, width // n_mp), bf),
             pltpu.VMEM((ff, cols), bf),
             pltpu.VMEM((cols, ff), bf),
             pltpu.VMEM((2 * high + 16, LANES), f32),
+            pltpu.VMEM((tok, width // n_mp), bf),
         ),
         in_specs=[anywhere] * 9,
-        out_specs=(anywhere,) + (vmem,) * 3,
+        out_specs=(vmem,) * 4,
         scratch_shapes=[
             pltpu.VMEM((2 * tok, width), bf),
             pltpu.VMEM((2 * tok, ff // 2), bf),
@@ -567,12 +558,10 @@
             pltpu.VMEM((n_dp * tok, cols), bf),
             pltpu.VMEM((cols, n_dp * tok), bf),
             pltpu.VMEM((slots, chunk, width), bf),
-            pltpu.VMEM((n_mp // 2, 2 * tok, width // n_mp), bf),
             pltpu.VMEM((n_mp, tok, width // n_mp), bf),
             pltpu.VMEM((cols, LANES), f32),
             pltpu.VMEM((3 * n_dp, high, LANES), f32),
             pltpu.VMEM((3 * n_mp, 8, LANES), f32),
-            pltpu.VMEM((tok, width // n_mp), bf),
             pltpu.VMEM((high, LANES), f32),
             pltpu.VMEM((low, LANES), f32),
             pltpu.VMEM((low, LANES), f32),
@@ -592,23 +581,23 @@
             ),
         )
     )
-    new_master_out, new_master_in = pl.pallas_call(
+    new_ig, new_master_out, new_master_in = pl.pallas_call(
         functools.partial(update_kernel, (ff, cols, tiles)),
-        out_shape=(shape((ff, cols), f32), shape((cols, ff), f32)),
-        in_specs=[vmem, anywhere, vmem, vmem, vmem],
-        out_specs=(anywhere,) * 2,
+        out_shape=(shape((tok, width // n_mp), bf), shape((ff, cols), f32), shape((cols, ff), f32)),
+        in_specs=[vmem] * 6,
+        out_specs=(anywhere,) * 3,
         scratch_shapes=[
             pltpu.VMEM((ff, cols), f32),
             pltpu.VMEM((cols, ff), f32),
-            pltpu.SemaphoreType.DMA((2, 2 * tiles)),
+            pltpu.SemaphoreType.DMA((2 * tiles + 1,)),
         ],
         compiler_params=pltpu.CompilerParams(vmem_limit_bytes=K2_VMEM),
-    )(in_vmem(master_out), in_hbm(master_in), *map(in_vmem, held))
-    return ig, new_master_in, new_master_out
-
-
-SEMAPHORES = 110
-K1_VMEM = 34 * 2**20
+    )(*map(in_vmem, (master_out, master_in, *held)))
+    return new_ig, new_master_in, new_master_out
+
+
+SEMAPHORES = 102
+K1_VMEM = 30 * 2**20
 K2_VMEM = 21 * 2**20
 PARTS = 6
 

time: 101 us -> 96.2 us (0.952)
  Pallas kernels: 99 us -> 95.2 us
    pallas_call x1, Pallas kernels: 88 us -> 85.8 us  [fast_body(): pl.pallas_call(functools.partial(step_kernel, plan), out_shape=(pltpu.VME...]
    pallas_call x1, Pallas kernels: 11 us -> 9.45 us  [fast_body(): pl.pallas_call(functools.partial(update_kernel, (ff, cols, tiles)), out_s...]
where the time goes in v3:
time: 96.2 us; the launch traced here: 96.1 us
  Pallas kernels  95.2 us (99%)
    pallas_call x1, Pallas kernels, fast_body(): pl.pallas_call(functools.partial(step_kernel, plan), out_shape=(pltpu.VME...  85.8 us
    pallas_call x1, Pallas kernels, fast_body(): pl.pallas_call(functools.partial(update_kernel, (ff, cols, tiles)), out_s...  9.45 us

profile of v3, /device:TPU:0, one launch (start us, length us, event | category | flops | bytes accessed | tf_op | source)
XLA Modules:
  0.0 96.1 jit_solution(3733161997579198332)
XLA Ops:
  0.6 0.0 copy-start
  0.6 0.0 copy-start.1
  0.7 85.8 %shard_map.130 = (bf16[3072,768]{1,0:T(8,128)(2,1)S(1)}, bf16[768,3072]{1,0:T(8,128)(2,1)S(1)}, f32[64,128]{1,0:T(8,128)S(1)}, bf16[128,1536]{1,0:T(8,128)(2,1)S(1)}) custom-call(bf16[128,6144]{1,0:T(8,128)(2,1)} %og_hbm.1, bf16[128,3072]{1,0:T(8,128)(2,1)} %pa_hbm.1, bf16[128,6144]{1,0:T(8,128)(2,1)} %in_hbm.1, bf16[3072,6144]{1,0:T(8,128)(2,1)} %wo_hbm.1, ...), custom_call_target="tpu_custom_call" | custom-call | tf_op jit(solution)/shard_map/pallas_call | solution.py:542
  86.4 0.0 copy-done
  86.5 0.0 copy-done.1
  86.5 9.4 %shard_map.131 = (bf16[128,1536]{1,0:T(8,128)(2,1)}, f32[3072,768]{1,0:T(8,128)}, f32[768,3072]{1,0:T(8,128)}) custom-call(f32[3072,768]{1,0:T(8,128)S(1)} %copy-done, f32[768,3072]{1,0:T(8,128)S(1)} %copy-done.1, bf16[3072,768]{1,0:T(8,128)(2,1)S(1)} %get-tuple-element.10.go, bf16[768,3072]{1,0:T(8,128)(2,1)S(1)} %get-tuple-element.11.gi, ...), custom_call_target="tpu_custom_call" | custom-call | tf_op jit(solution)/shard_map/pallas_call | solution.py:584
Async XLA Ops:
  0.6 85.8 %copy-start = (f32[3072,768]{1,0:T(8,128)S(1)}, f32[3072,768]{1,0:T(8,128)}, u32[]{:S(2)}) copy-start(f32[3072,768]{1,0:T(8,128)} %mo.1) | copy-start | bytes 28311556
  0.6 85.8 %copy-start.1 = (f32[768,3072]{1,0:T(8,128)S(1)}, f32[768,3072]{1,0:T(8,128)}, u32[]{:S(2)}) copy-start(f32[768,3072]{1,0:T(8,128)} %mi.1) | copy-start | bytes 28311556

commit v4 on v3

--- a/solution.py
+++ b/solution.py
@@ -494,34 +494,42 @@
     c.drain()
 
 
-def update_kernel(plan, mo, mi, go, gi, fac, ig, new_ig, new_out, new_in, out_b, in_b, sems):
-    ff, cols, tiles = plan
+def update_kernel(plan, mo, mi, go, gi, fac, ig, new_ig, new_out, new_in, out_b, in_b, downs, sems):
+    ff, cols = plan
     high, low = ff // LANES, cols // LANES
-    stores = [pltpu.make_async_copy(ig, new_ig, sems.at[2 * tiles])]
-    stores[0].start()
+    whole = [
+        pltpu.make_async_copy(ig, new_ig, sems.at[0]),
+        pltpu.make_async_copy(out_b, new_out, sems.at[1]),
+        pltpu.make_async_copy(in_b, new_in, sems.at[2]),
+    ]
+    whole[0].start()
     turned = fac[...].T
-    for new, old, stage, grad, first, height, across, rows_at, cols_at in (
-        (new_out, mo, out_b, go, 0, high, low, 0, 2 * high),
-        (new_in, mi, in_b, gi, tiles, low, high, 2 * high + 8, high),
-    ):
-        for tile in range(tiles):
-            bands = range(tile * height // tiles, (tile + 1) * height // tiles)
-            for band in bands:
-                rows = slice(band * LANES, (band + 1) * LANES)
-                down = jnp.broadcast_to(turned[:, rows_at + band : rows_at + band + 1], (LANES, LANES))
-
-                def lane_group(j, carry):
-                    at = pl.ds(pl.multiple_of(j * LANES, LANES), LANES)
-                    scale = down * fac[pl.ds(cols_at + j, 1), :]
+    for at, column in enumerate((*range(high), *range(2 * high + 8, 2 * high + 8 + low))):
+        downs[at] = jnp.broadcast_to(turned[:, column : column + 1], (LANES, LANES))
+
+    def update(new, old, stage, grad, sem, first, group, groups, cols_at):
+        def band(b, carry):
+            rows = pl.ds(pl.multiple_of(b * LANES, LANES), LANES)
+            down = downs[first + b]
+
+            def lane_groups(g, carry):
+                for j in range(group):
+                    at = pl.ds(pl.multiple_of((g * group + j) * LANES, LANES), LANES)
+                    scale = down * fac[pl.ds(cols_at + g * group + j, 1), :]
                     stage[rows, at] = old[rows, at] - grad[rows, at].astype(jnp.float32) * scale
-                    return carry
-
-                lax.fori_loop(0, across, lane_group, 0, unroll=3)
-            rows = slice(bands[0] * LANES, (bands[-1] + 1) * LANES)
-            stores.append(pltpu.make_async_copy(stage.at[rows], new.at[rows], sems.at[first + tile]))
-            stores[-1].start()
-    for store in stores:
-        store.wait()
+                return carry
+
+            lax.fori_loop(0, groups, lane_groups, 0)
+            pltpu.make_async_copy(stage.at[rows], new.at[rows], sems.at[sem]).start()
+            return carry
+
+        lax.fori_loop(0, stage.shape[0] // LANES, band, 0)
+
+    group = math.gcd(high, low)
+    update(new_out, mo, out_b, go, 1, 0, group, low // group, 2 * high)
+    update(new_in, mi, in_b, gi, 2, high, group, high // group, high)
+    for copy in whole:
+        copy.wait()
 
 
 def fast_body(n_dp, n_mp, inputs, pre_act, out_grad, w_in, w_out, master_in, master_out, row_in, col_in, row_out, col_out):
@@ -531,7 +539,7 @@
     parts = PARTS
     chunk = ff // 2 // parts
     high, low = ff // LANES, cols // LANES
-    slots, tiles = 2, math.gcd(high, low)
+    slots = 2
     bf, f32 = jnp.bfloat16, jnp.float32
     anywhere = pl.BlockSpec(memory_space=pl.ANY)
     vmem = pl.BlockSpec(memory_space=pltpu.VMEM)
@@ -582,14 +590,15 @@
         )
     )
     new_ig, new_master_out, new_master_in = pl.pallas_call(
-        functools.partial(update_kernel, (ff, cols, tiles)),
+        functools.partial(update_kernel, (ff, cols)),
         out_shape=(shape((tok, width // n_mp), bf), shape((ff, cols), f32), shape((cols, ff), f32)),
         in_specs=[vmem] * 6,
         out_specs=(anywhere,) * 3,
         scratch_shapes=[
             pltpu.VMEM((ff, cols), f32),
             pltpu.VMEM((cols, ff), f32),
-            pltpu.SemaphoreType.DMA((2 * tiles + 1,)),
+            pltpu.VMEM((high + low, LANES, LANES), f32),
+            pltpu.SemaphoreType.DMA((3,)),
         ],
         compiler_params=pltpu.CompilerParams(vmem_limit_bytes=K2_VMEM),
     )(*map(in_vmem, (master_out, master_in, *held)))

time: 96.2 us -> 94 us (0.977)
  Pallas kernels: 95.2 us -> 93.1 us
    pallas_call x1, Pallas kernels: 9.45 us -> 7.27 us  [fast_body(): pl.pallas_call(functools.partial(update_kernel, (ff, cols)), out_shape=(s...]
where the time goes in v4:
time: 94 us; the launch traced here: 93.9 us
  Pallas kernels  93.1 us (99%)
    pallas_call x1, Pallas kernels, fast_body(): pl.pallas_call(functools.partial(step_kernel, plan), out_shape=(pltpu.VME...  85.8 us
    pallas_call x1, Pallas kernels, fast_body(): pl.pallas_call(functools.partial(update_kernel, (ff, cols)), out_shape=(s...  7.27 us

profile of v4, /device:TPU:0, one launch (start us, length us, event | category | flops | bytes accessed | tf_op | source)
XLA Modules:
  0.0 93.9 jit_solution(17025411752539326861)
XLA Ops:
  0.6 0.0 copy-start
  0.6 0.0 copy-start.1
  0.7 85.8 %shard_map.130 = (bf16[3072,768]{1,0:T(8,128)(2,1)S(1)}, bf16[768,3072]{1,0:T(8,128)(2,1)S(1)}, f32[64,128]{1,0:T(8,128)S(1)}, bf16[128,1536]{1,0:T(8,128)(2,1)S(1)}) custom-call(bf16[128,6144]{1,0:T(8,128)(2,1)} %og_hbm.1, bf16[128,3072]{1,0:T(8,128)(2,1)} %pa_hbm.1, bf16[128,6144]{1,0:T(8,128)(2,1)} %in_hbm.1, bf16[3072,6144]{1,0:T(8,128)(2,1)} %wo_hbm.1, ...), custom_call_target="tpu_custom_call" | custom-call | tf_op jit(solution)/shard_map/pallas_call | solution.py:550
  86.4 0.0 copy-done
  86.5 0.0 copy-done.1
  86.5 7.3 %shard_map.131 = (bf16[128,1536]{1,0:T(8,128)(2,1)}, f32[3072,768]{1,0:T(8,128)}, f32[768,3072]{1,0:T(8,128)}) custom-call(f32[3072,768]{1,0:T(8,128)S(1)} %copy-done, f32[768,3072]{1,0:T(8,128)S(1)} %copy-done.1, bf16[3072,768]{1,0:T(8,128)(2,1)S(1)} %get-tuple-element.10.go, bf16[768,3072]{1,0:T(8,128)(2,1)S(1)} %get-tuple-element.11.gi, ...), custom_call_target="tpu_custom_call" | custom-call | tf_op jit(solution)/shard_map/pallas_call | solution.py:592
Async XLA Ops:
  0.6 85.8 %copy-start = (f32[3072,768]{1,0:T(8,128)S(1)}, f32[3072,768]{1,0:T(8,128)}, u32[]{:S(2)}) copy-start(f32[3072,768]{1,0:T(8,128)} %mo.1) | copy-start | bytes 28311556
  0.6 85.8 %copy-start.1 = (f32[768,3072]{1,0:T(8,128)S(1)}, f32[768,3072]{1,0:T(8,128)}, u32[]{:S(2)}) copy-start(f32[768,3072]{1,0:T(8,128)} %mi.1) | copy-start | bytes 28311556
